TPU v7x, 128 devices: a whole 4x4x4 slice. The times are simulated.
128 devices in a mesh: section: 2 (over x_hi), grp: 64 (over y, z, x_lo, core).
Axes of the slice: x: 4 (x_hi: 2, x_lo: 2; x = x_hi * 2 + x_lo), y: 4, z: 4, core: 2. Of those that a mesh axis runs over, the one named last changes fastest.
Arguments:
- voltages: bfloat16 [1024, 524288], P('grp', 'section'), may hold values from -6 to 6
- filter_taps: float32 [8, 512], replicated, may hold values from -2 to 2
- beam_weights: bfloat16 [256, 2, 512, 1024], P('grp'), may hold values from -0.125 to 0.125
- antenna_of_row: int32 [1024], replicated, may hold values from 0 to 1023, each once
- beam_delay: int32 [512], P('grp'), may hold values from 0 to 127
Outputs:
- dedispersed: float32 [256, 2, 512, 1024], P(None, None, 'grp', 'section')
Inputs may be any that keep to these rules, and one draw needn't show every extreme that they name: A permutation: voltage row r holds physical antenna antenna_of_row[r].
All inputs are finite; a program needn't handle non-finite values.
Results may differ from a plain program's by a relative error of at most 0.0069.
Values may be sent and summed in bfloat16 or wider, within the bound.
A program may use at most 128 MiB of HBM per device.

v0:
```python
import math

import jax
import jax.numpy as jnp
from jax import lax
from jax.sharding import PartitionSpec as P

DFT_LEN = 256


def shifted(value, axis, steps):
    count = lax.axis_size(axis)
    leading, last = (max(0, -steps), min(count, count - steps))
    return lax.ppermute(value, axis, [(source, source + steps) for source in range(leading, last)])


def dft_table(frame_length, group_count, split_ways):
    channels = frame_length // 2
    per_target = channels // (group_count * split_ways)
    column = jnp.arange(frame_length, dtype=jnp.int32)
    target = column // (2 * per_target)
    within = column % (2 * per_target)
    quadrature = within // per_target
    channel = (
        target % group_count * (per_target * split_ways)
        + target // group_count * per_target
        + within % per_target
    )
    sample = jnp.arange(frame_length, dtype=jnp.int32)[:, None]
    winding = sample * channel[None, :] % frame_length
    angles = 2.0 * math.pi / frame_length * winding.astype(jnp.float32)
    factor = channels ** (-0.5)
    dft_cols = jnp.where(
        quadrature[None, :] == 0, jnp.cos(angles) * factor, -jnp.sin(angles) * factor
    )
    return dft_cols.astype(jnp.bfloat16)


def block_tables(length):
    half_len = length // 2
    factor = length ** (-0.5)
    sample = jnp.arange(length, dtype=jnp.int32)
    angles = (
        2.0 * math.pi / length * (sample[:, None] * sample[None, :] % length).astype(jnp.float32)
    )
    cosine_table = (jnp.cos(angles) * factor).astype(jnp.bfloat16)
    sine_table = (jnp.sin(angles) * factor).astype(jnp.bfloat16)
    forward_real = jnp.concatenate([cosine_table, -sine_table], axis=1)
    forward_imag = jnp.concatenate([sine_table, cosine_table], axis=1)
    back_cos = cosine_table[:, half_len:]
    back_sin = sine_table[:, half_len:]
    inverse_real = jnp.concatenate([back_cos, back_sin], axis=1)
    inverse_imag = jnp.concatenate([-back_sin, back_cos], axis=1)
    return (forward_real, forward_imag, inverse_real, inverse_imag)


def chirp_factor(delays, channel_count, channels, length):
    frequency = jnp.arange(length, dtype=jnp.int32)
    signed = jnp.where(frequency < length // 2, frequency, frequency - length).astype(jnp.float32)
    channel = jnp.arange(channel_count, dtype=jnp.int32).astype(jnp.float32)
    strength = (1.0 + channel / channels) ** (-3.0)
    sweep = signed * signed / (length * length)
    phases = (math.pi * delays.astype(jnp.float32))[None, :, None] * strength[
        :, None, None
    ] * sweep[None, None, :] - 0.5 * math.pi * frequency.astype(jnp.float32)[None, None, :]
    return (jnp.cos(phases), jnp.sin(phases))


def dedisperse(series, leading, delays, tables, channels):
    forward_real, forward_imag, inverse_real, inverse_imag = tables
    length = forward_real.shape[0]
    advance = length // 2
    chan_count = series.shape[0]
    beam_count = series.shape[2]
    time_len = series.shape[3]
    block_count = time_len // advance
    joined = jnp.concatenate([leading, series], axis=3).reshape(
        chan_count, 2, beam_count, block_count + 1, advance
    )
    blocks = jnp.concatenate([joined[:, :, :, :-1, :], joined[:, :, :, 1:, :]], axis=4)
    spectrum = jnp.einsum(
        "cbml,lk->cbmk", blocks[:, 0], forward_real, preferred_element_type=jnp.float32
    ) + jnp.einsum("cbml,lk->cbmk", blocks[:, 1], forward_imag, preferred_element_type=jnp.float32)
    chirp_real, chirp_imag = chirp_factor(delays, chan_count, channels, length)
    chirp_real = chirp_real[:, :, None, :]
    chirp_imag = chirp_imag[:, :, None, :]
    spec_real = spectrum[..., :length]
    spec_imag = spectrum[..., length:]
    filtered_real = (spec_real * chirp_real - spec_imag * chirp_imag).astype(jnp.bfloat16)
    filtered_imag = (spec_real * chirp_imag + spec_imag * chirp_real).astype(jnp.bfloat16)
    result = jnp.einsum(
        "cbmk,kn->cbmn", filtered_real, inverse_real, preferred_element_type=jnp.float32
    ) + jnp.einsum("cbmk,kn->cbmn", filtered_imag, inverse_imag, preferred_element_type=jnp.float32)
    out_real = result[..., :advance].reshape(chan_count, beam_count, time_len)
    out_imag = result[..., advance:].reshape(chan_count, beam_count, time_len)
    return jnp.stack([out_real, out_imag], axis=1)


def local(voltages, filter_taps, beam_weights, antenna_of_row, beam_delay):
    group_count = lax.axis_size("grp")
    antenna_row_set = voltages.shape[0]
    samples = voltages.shape[1]
    filter_tap_count = filter_taps.shape[0]
    frame_length = filter_taps.shape[1]
    channel_spectra = samples // frame_length
    channels = frame_length // 2
    antennas = antenna_of_row.shape[0]
    beam_count = beam_weights.shape[2]
    past_samples = shifted(
        voltages[:, samples - (filter_tap_count - 1) * frame_length :], "section", 1
    )
    extended = jnp.concatenate([past_samples, voltages], axis=1).reshape(
        antenna_row_set, channel_spectra + filter_tap_count - 1, frame_length
    )
    weighted = filter_taps[0] * extended[:, 0:channel_spectra, :]
    for tap_index in range(1, filter_tap_count):
        weighted = (
            weighted
            + filter_taps[tap_index] * extended[:, tap_index : tap_index + channel_spectra, :]
        )
    weighted = weighted.astype(jnp.bfloat16)
    split_ways = 1
    dft_cols = dft_table(frame_length, group_count, split_ways)
    channelised = jnp.einsum(
        "asp,pj->ajs", weighted, dft_cols, preferred_element_type=jnp.float32
    ).astype(jnp.bfloat16)[None]
    per_target = channels // (group_count * split_ways)
    ordered = jnp.take(beam_weights, antenna_of_row, axis=3).reshape(
        per_target, 2 * beam_count, antennas
    )
    tables = block_tables(DFT_LEN)
    received = lax.all_to_all(channelised, "grp", split_axis=2, concat_axis=0, tiled=True)
    item_count = received.shape[3]
    halves = received.shape[0] * received.shape[1] // antennas
    all_rows = received.reshape(halves, antennas, 2 * per_target, item_count)
    with_real = jnp.einsum(
        "cba,hacs->cbhs",
        ordered,
        all_rows[:, :, :per_target, :],
        preferred_element_type=jnp.float32,
    )
    with_imag = jnp.einsum(
        "cba,hacs->cbhs",
        ordered,
        all_rows[:, :, per_target:, :],
        preferred_element_type=jnp.float32,
    )
    beam_real = with_real[:, :beam_count] - with_imag[:, beam_count:]
    beam_imag = with_imag[:, :beam_count] + with_real[:, beam_count:]
    formed = jnp.stack([beam_real, beam_imag], axis=1).astype(jnp.bfloat16)
    arrival_buffer = lax.all_to_all(
        formed.reshape(per_target, 2, beam_count, channel_spectra),
        "grp",
        split_axis=2,
        concat_axis=0,
        tiled=True,
    )
    leading = shifted(arrival_buffer[:, :, :, channel_spectra - DFT_LEN // 2 :], "section", 1)
    result = dedisperse(arrival_buffer, leading, beam_delay, tables, channels)
    return result


def solution(mesh):
    in_specs = (P("grp", "section"), P(), P("grp", None, None, None), P(), P("grp"))
    out_specs = P(None, None, "grp", "section")
    return jax.shard_map(local, mesh=mesh, in_specs=in_specs, out_specs=out_specs, check_vma=False)
```

profile of v0, /device:TPU:70, one launch (start us, length us, event | category | flops | bytes accessed | tf_op | source)
XLA Modules:
  0.0 427.6 jit_solution(12808330259375173368)
XLA Ops:
  9.2 7.2 %pad_maximum_fusion = bf16[16,265728]{1,0:T(8,128)(2,1)} fusion(bf16[16,262144]{1,0:T(8,128)(2,1)} %param.5, bf16[16,3584]{1,0:T(8,128)(2,1)S(1)} %collective-permute-done), kind=kLoop, calls=%fused_computation.3 | loop fusion | flops 17006592 | bytes 17006592 | tf_op jit(solution)/shard_map/concatenate | solution.py:112
  16.4 12.4 %reshape.188 = bf16[16,519,512]{2,1,0:T(8,128)(2,1)} reshape(bf16[16,265728]{1,0:T(8,128)(2,1)} %pad_maximum_fusion) | data formatting | bytes 17006592 | tf_op jit(solution)/shard_map/reshape | solution.py:112
  28.7 44.7 %convert_bitcast_fusion = bf16[1,16,512,512]{3,2,1,0:T(8,128)(2,1)} fusion(bf16[16,519,512]{2,1,0:T(8,128)(2,1)} %reshape.188, f32[512]{0:T(512)S(1)} %bitcast.97, f32[512]{0:T(512)S(1)} %bitcast.98, f32[512]{0:T(512)S(1)} %bitcast.92, f32[512]{0:T(512)S(1)} %bitcast.93, f32[512]{0:T(512)S(1)} %bitcast.94, f32[512]{0:T(512)S(1)} %bitcast.95, ...), kind=kOutput, calls=%fused_computation.8 | convolution fusion | flops 4399824896 | bytes 76038144 | tf_op jit(solution)/shard_map/asp,pj->ajs/dot_general | solution.py:124
  73.4 11.4 %copy.43 = bf16[1,16,512,512]{3,1,0,2:T(8,128)(2,1)} copy(bf16[1,16,512,512]{3,2,1,0:T(8,128)(2,1)} %convert_bitcast_fusion) | data formatting | bytes 16777216 | tf_op jit(solution)/shard_map/broadcast_in_dim | solution.py:124
  84.8 9.8 %all-to-all-start = ((bf16[1,16,512,512]{3,1,0,2:T(8,128)(2,1)}), bf16[1,16,512,512]{3,1,0,2:T(8,128)(2,1)}, u32[]{:S(2)}, u32[]{:S(2)}) async-start(bf16[1,16,512,512]{3,1,0,2:T(8,128)(2,1)} %copy.43), calls=%async_computation | async-start | bytes 16777216 | tf_op jit(solution)/shard_map/all_to_all | solution.py:132
  94.6 14.8 %copy.41 = bf16[4,2,512,1024]{2,0,3,1:T(4,128)(2,1)} copy(bf16[4,2,512,1024]{3,2,1,0:T(8,128)(2,1)} %param.7) | data formatting | bytes 16777216 | tf_op args[2]
  109.4 19.0 %gather_fusion = bf16[1024,4,2,512]{3,1,2,0:T(4,128)(2,1)} fusion(bf16[4,2,512,1024]{2,0,3,1:T(4,128)(2,1)} %copy.41, s32[1024]{0:T(1024)S(1)} %fusion.49), kind=kCustom, calls=%fused_computation | custom fusion | bytes 16781312 | tf_op jit(solution)/shard_map/jit(_take)/gather | solution.py:128
  128.4 13.7 %copy.42 = bf16[4,2,512,1024]{3,2,1,0:T(8,128)(2,1)} copy(bf16[4,2,512,1024]{2,0,1,3:T(4,128)(2,1)} %bitcast.81) | data formatting | bytes 16777216 | tf_op jit(solution)/shard_map/jit(_take)/gather | solution.py:128
  142.1 7.3 %bitcast_select_fusion = bf16[4,1024,1024]{2,1,0:T(8,128)(2,1)} fusion(bf16[4,2,512,1024]{3,2,1,0:T(8,128)(2,1)} %copy.42, pred[1024]{0:T(1024)(128)(4,1)S(1)} %compare_and_fusion), kind=kLoop, calls=%fused_computation.5 | loop fusion | flops 4194304 | bytes 16778240 | tf_op jit(solution)/shard_map/jit(_take)/select_n | solution.py:128
  149.4 62.7 %all-to-all-done = bf16[1,16,512,512]{3,1,0,2:T(8,128)(2,1)} async-done(((bf16[1,16,512,512]{3,1,0,2:T(8,128)(2,1)}), bf16[1,16,512,512]{3,1,0,2:T(8,128)(2,1)}, u32[]{:S(2)}, u32[]{:S(2)}) %all-to-all-start) | async-done | bytes 8388640 | tf_op jit(solution)/shard_map/all_to_all | solution.py:132
  212.1 8.3 %copy.44 = bf16[1,16,64,8,512]{4,1,2,3,0:T(8,128)(2,1)} copy(bf16[1,16,64,8,512]{4,1,3,2,0:T(8,128)(2,1)} %bitcast.13) | data formatting | bytes 16777216 | tf_op jit(solution)/shard_map/all_to_all | solution.py:132
  220.5 8.3 %fusion.12 = f32[4,1024,1,512]{3,1,0,2:T(8,128)S(1)} fusion(bf16[4,1024,1024]{2,1,0:T(8,128)(2,1)} %bitcast_select_fusion, bf16[1,1024,8,512]{3,1,2,0:T(8,128)(2,1)} %bitcast.89), kind=kOutput, calls=%fused_computation.32 | convolution fusion | flops 4294967296 | bytes 20971520 | tf_op jit(solution)/shard_map/cba,hacs->cbhs/dot_general | solution.py:136
  228.8 9.0 %fusion.13 = f32[4,1024,1,512]{3,1,0,2:T(8,128)} fusion(bf16[4,1024,1024]{2,1,0:T(8,128)(2,1)S(1)} %bitcast.88, bf16[1,1024,8,512]{3,1,2,0:T(8,128)(2,1)} %bitcast.90), kind=kOutput, calls=%fused_computation.33 | convolution fusion | flops 4294967296 | bytes 20971520 | tf_op jit(solution)/shard_map/cba,hacs->cbhs/dot_general | solution.py:142
  247.7 9.0 %all-to-all-start.1 = ((bf16[4,2,512,512]{3,0,1,2:T(4,128)(2,1)}), bf16[4,2,512,512]{3,0,1,2:T(4,128)(2,1)}, u32[]{:S(2)}, u32[]{:S(2)}) async-start(bf16[4,2,512,512]{3,0,1,2:T(4,128)(2,1)} %copy.45), calls=%async_computation.1 | async-start | bytes 8388608 | tf_op jit(solution)/shard_map/all_to_all | solution.py:151
  258.8 52.8 %all-to-all-done.1 = bf16[4,2,512,512]{3,0,1,2:T(4,128)(2,1)} async-done(((bf16[4,2,512,512]{3,0,1,2:T(4,128)(2,1)}), bf16[4,2,512,512]{3,0,1,2:T(4,128)(2,1)}, u32[]{:S(2)}, u32[]{:S(2)}) %all-to-all-start.1) | async-done | bytes 4194336 | tf_op jit(solution)/shard_map/all_to_all | solution.py:151
  317.5 7.4 %fusion.18 = (f32[256,8,256]{2,0,1:T(8,128)S(1)}, f32[256,8,256]{2,0,1:T(8,128)S(1)}) fusion(f32[256]{0:T(256)S(1)} %get-tuple-element.26, f32[256]{0:T(256)S(1)} %get-tuple-element.25, f32[256,8]{0,1:T(8,128)S(1)} %broadcast_multiply_fusion), kind=kLoop, calls=%fused_computation.39 | loop fusion | flops 1048576 | bytes 4204544 | tf_op jit(solution)/shard_map/cos | solution.py:66
  324.9 19.2 %collective-permute-done.1 = bf16[256,2,8,128]{3,2,1,0:T(8,128)(2,1)S(1)} collective-permute-done((bf16[256,2,8,128]{3,2,1,0:T(8,128)(2,1)S(1)}, bf16[256,2,8,128]{3,2,1,0:T(8,128)(2,1)S(1)}, u32[]{:S(2)}, u32[]{:S(2)}) %collective-permute-start.1) | collective-permute-done | bytes 1048608 | tf_op jit(solution)/shard_map/ppermute | solution.py:14
  353.9 8.1 %fusion.3 = f32[256,8,4,512]{3,0,2,1:T(8,128)} fusion(bf16[256,2,8,4,256]{4,0,3,2,1:T(8,128)(2,1)S(1)} %copy_dynamic-update-slice_fusion, bf16[256,256]{1,0:T(8,128)(2,1)S(1)} %fusion.48, bf16[256,256]{1,0:T(8,128)(2,1)S(1)} %get-tuple-element.24), kind=kOutput, calls=%fused_computation.15 | convolution fusion | flops 2148007936 | bytes 21233664 | tf_op jit(solution)/shard_map/cbml,lk->cbmk/dot_general | solution.py:81
  362.0 13.9 %convolution_add_fusion = f32[256,8,4,512]{3,0,2,1:T(8,128)} fusion(f32[256,8,4,512]{3,0,2,1:T(8,128)} %fusion.3, bf16[256,2,8,4,256]{4,0,3,2,1:T(8,128)(2,1)S(1)} %copy_dynamic-update-slice_fusion, bf16[256,256]{1,0:T(8,128)(2,1)S(1)} %get-tuple-element.24, bf16[256,256]{1,0:T(8,128)(2,1)S(1)} %get-tuple-element.23), kind=kOutput, calls=%fused_computation.2 | convolution fusion | flops 2152202240 | bytes 38010880 | tf_op jit(solution)/shard_map/cbml,lk->cbmk/dot_general | solution.py:83
  375.9 10.9 %fusion.1 = f32[256,8,4,256]{0,3,2,1:T(8,128)} fusion(f32[256,8,4,512]{3,0,2,1:T(8,128)} %convolution_add_fusion, f32[256,8,256]{2,0,1:T(8,128)S(1)} %get-tuple-element.22, f32[256,8,256]{2,0,1:T(8,128)S(1)} %get-tuple-element.21, bf16[256,128]{1,0:T(8,128)(2,1)S(1)} %get-tuple-element.12, bf16[256,128]{1,0:T(8,128)(2,1)S(1)} %slice.163), kind=kOutput, calls=%fused_computation.11 | convolution fusion | flops 1082392576 | bytes 29491200 | tf_op jit(solution)/shard_map/cbmk,kn->cbmn/dot_general | solution.py:91
  386.8 13.5 %fusion.14 = f32[256,8,4,256]{0,3,2,1:T(8,128)} fusion(f32[256,8,4,256]{0,3,2,1:T(8,128)} %fusion.1, f32[256,8,4,512]{3,0,2,1:T(8,128)} %convolution_add_fusion, f32[256,8,256]{2,0,1:T(8,128)S(1)} %get-tuple-element.22, f32[256,8,256]{2,0,1:T(8,128)S(1)} %get-tuple-element.21, bf16[256,128]{1,0:T(8,128)(2,1)S(1)} %slice.163, ...), kind=kOutput, calls=%fused_computation.34 | convolution fusion | flops 1084489728 | bytes 37879808 | tf_op jit(solution)/shard_map/cbmk,kn->cbmn/dot_general | solution.py:93
  400.2 7.7 %fusion.78 = (f32[256,8,4,128]{0,3,2,1:T(8,128)}, f32[256,8,4,128]{0,3,2,1:T(8,128)}) fusion(f32[256,8,4,256]{0,3,2,1:T(8,128)} %fusion.14), kind=kLoop, calls=%fused_computation.136 | loop fusion | bytes 16777216 | tf_op jit(solution)/shard_map/slice | solution.py:94
  407.9 5.6 %copy.52 = f32[256,1,8,512]{3,2,1,0:T(8,128)} copy(f32[256,1,8,512]{0,3,2,1:T(8,128)} %bitcast.86) | data formatting | bytes 8388608 | tf_op jit(solution)/shard_map/stack;reshape | solution.py:96
  419.1 8.1 %pad_maximum_fusion.1 = f32[256,2,8,512]{3,2,1,0:T(8,128)} fusion(f32[256,1,8,512]{3,2,1,0:T(8,128)} %copy.53, f32[256,1,8,512]{3,2,1,0:T(8,128)} %copy.52), kind=kLoop, calls=%fused_computation.4 | loop fusion | flops 2097152 | bytes 16777216 | tf_op jit(solution)/shard_map/stack | solution.py:96
  (38 shorter events, 42.3 us)
Async XLA Ops:
  0.9 8.3 %collective-permute-start = (bf16[16,3584]{1,0:T(8,128)(2,1)S(1)}, bf16[16,3584]{1,0:T(8,128)(2,1)S(1)}, u32[]{:S(2)}, u32[]{:S(2)}) collective-permute-start(bf16[16,3584]{1,0:T(8,128)(2,1)S(1)} %slice.107), channel_id=1, source_target_pairs={{0,64},{1,65},{2,66},{3,67},{4,68},{5,69},{6,70},{7,71},{8,72},{9,... | collective-permute-start | bytes 344072 | tf_op jit(solution)/shard_map/ppermute | solution.py:14
  84.8 127.4 %all-to-all-start = ((bf16[1,16,512,512]{3,1,0,2:T(8,128)(2,1)}), bf16[1,16,512,512]{3,1,0,2:T(8,128)(2,1)}, u32[]{:S(2)}, u32[]{:S(2)}) async-start(bf16[1,16,512,512]{3,1,0,2:T(8,128)(2,1)} %copy.43), calls=%async_computation | async-start | bytes 16777216 | tf_op jit(solution)/shard_map/all_to_all | solution.py:132
  94.6 14.8 %copy-start = (s32[1024]{0:T(1024)S(1)}, s32[1024]{0:T(1024)}, u32[]{:S(2)}) copy-start(s32[1024]{0:T(1024)} %param.8) | copy-start | bytes 12292
  212.1 16.6 %slice-start = ((s8[8388608]{0:T(1024)(128)(4,1)}), s8[4194304]{0:T(1024)(128)(4,1)S(1)}, s32[]{:S(2)}) async-start(s8[8388608]{0:T(1024)(128)(4,1)} %bitcast.87), calls=%async_computation.2 | async-start | bytes 8388608
  220.5 8.3 %slice-start.1 = ((s8[8388608]{0:T(1024)(128)(4,1)}), s8[4194304]{0:T(1024)(128)(4,1)S(1)}, s32[]{:S(2)}) async-start(s8[8388608]{0:T(1024)(128)(4,1)} %bitcast.87), calls=%async_computation.3 | async-start | bytes 8388608
  247.7 64.0 %all-to-all-start.1 = ((bf16[4,2,512,512]{3,0,1,2:T(4,128)(2,1)}), bf16[4,2,512,512]{3,0,1,2:T(4,128)(2,1)}, u32[]{:S(2)}, u32[]{:S(2)}) async-start(bf16[4,2,512,512]{3,0,1,2:T(4,128)(2,1)} %copy.45), calls=%async_computation.1 | async-start | bytes 8388608 | tf_op jit(solution)/shard_map/all_to_all | solution.py:151
  258.8 58.5 %copy-start.1 = (s32[8]{0:T(128)S(1)}, s32[8]{0:T(128)}, u32[]{:S(2)}) copy-start(s32[8]{0:T(128)} %param.9) | copy-start | bytes 100
  316.0 28.0 %collective-permute-start.1 = (bf16[256,2,8,128]{3,2,1,0:T(8,128)(2,1)S(1)}, bf16[256,2,8,128]{3,2,1,0:T(8,128)(2,1)S(1)}, u32[]{:S(2)}, u32[]{:S(2)}) collective-permute-start(bf16[256,2,8,128]{3,2,1,0:T(8,128)(2,1)S(1)} %slice.156), channel_id=1, source_target_pairs={{0,64},{1,65},{2,66},{3,67},{4,68},{5,69},{6,70},{7,71},{8,72},{9,... | collective-permute-start | bytes 3145736 | tf_op jit(solution)/shard_map/ppermute | solution.py:14
where the time goes:
time: 436 us; the launch traced here: 428 us
  waiting for transfers between devices  136 us (31%)
  local copies, waits for them, and re-layouts  119 us (27%)
  matrix products  108 us (25%)
  other arithmetic  43.1 us (10%)
  starting transfers between devices  21.4 us (5%)
    all_to_all x1, waiting for transfers between devices, local(): lax.all_to_all(channelised, 'grp', split_axis=2, concat_axis=0, tiled=True)  62.7 us
    all_to_all x1, waiting for transfers between devices, local(): lax.all_to_all(formed.reshape(per_target, 2, beam_count, channel_spectra)...  52.8 us
    dot_general x1, matrix products, local(): jnp.einsum('asp,pj->ajs', weighted, dft_cols, preferred_element_type=jnp....  44.7 us
    gather x2, local copies, waits for them, and re-layouts, local(): jnp.take(beam_weights, antenna_of_row, axis=3)  32.6 us
    ppermute x2, waiting for transfers between devices, shifted(): lax.ppermute(value, axis, [(source, source + steps) for source in range(l...  20 us
    unnamed x10, local copies, waits for them, and re-layouts  17.5 us
    dot_general x1, matrix products, dedisperse(): jnp.einsum('cbml,lk->cbmk', blocks[:, 1], forward_imag, preferred_element...  13.9 us
    dot_general x1, matrix products, dedisperse(): jnp.einsum('cbmk,kn->cbmn', filtered_imag, inverse_imag, preferred_elemen...  13.5 us
  transfers between devices with their start and end apart: 4, of which 4 were waited for; matrix products, arithmetic and copies ran while one was open for 16% of the time, Pallas kernels for 0%

commit v1 on v0

v1 whole, which is shorter than its diff:
```python
import functools
import math
import random

import jax
import jax.numpy as jnp
import numpy as np
from jax import lax
from jax.experimental import pallas as pl
from jax.experimental.pallas import tpu as pltpu
from jax.sharding import PartitionSpec as P

MESH = pl.DeviceIdType.MESH
F32 = jnp.float32
BF16 = jnp.bfloat16
NG = 64
NY, NZ, NX, NC = 4, 4, 2, 2
ANT = 16
FRAME = 512
HALF = FRAME // 2
TAPS = 8
CH = 256
CPD = CH // NG
CHUNKS = 4
SC = 128
LEAD = (TAPS - 1) * FRAME
BEAMS = 512
BPD = BEAMS // NG
ROWS = CH * BPD
ALL_ANT = ANT * NG
RT = 256


def send_order(seed=0):
    rng = random.Random(seed)
    left = [
        (dy, dz, dx, dc) for dy in range(NY) for dz in range(NZ) for dx in range(NX) for dc in range(NC)
    ][1:]
    rng.shuffle(left)
    load = {}

    def ports(o):
        p = []
        for name, d in (("y", o[0]), ("z", o[1])):
            if d in (1, 2):
                p.append(name + "+")
            if d in (2, 3):
                p.append(name + "-")
        if o[2]:
            p.append("x")
        return p

    out = []
    while left:
        best = min(
            left,
            key=lambda o: (max([load.get(p, 0) + 1 for p in ports(o)] + [0]), -len(ports(o)), rng.random()),
        )
        for p in ports(best):
            load[p] = load.get(p, 0) + 1
        out.append(best)
        left.remove(best)
    return out


ORDER = send_order()


def channel_tables():
    j = np.arange(256)
    p = np.arange(HALF)
    tables = []
    for odd in (0, 1):
        channel = (j // 4) * CPD + ((j // 2) % 2) * 2 + odd
        angle = 2.0 * np.pi * ((channel[:, None] * p[None, :]) % FRAME) / FRAME
        value = np.where((j % 2)[:, None] == 0, np.cos(angle), -np.sin(angle)) / math.sqrt(CH)
        tables.append(value.astype(np.float32))
    return np.concatenate(tables, axis=0)


def block_tables():
    n = np.arange(2 * SC)
    angle = 2.0 * np.pi * ((n[:, None] * n[None, :]) % (2 * SC)) / (2 * SC)
    factor = 1.0 / math.sqrt(2 * SC)
    return np.stack([np.cos(angle) * factor, np.sin(angle) * factor]).astype(np.float32)


def kernel(
    volt, taps, weights, ant_row, delay, chan_tab, blk_tab,
    out,
    vbuf, halo_a, wblk, wrow, chan, send_a, recv_a, perm, onehot, wstage, wperm,
    btmp, send_b, recv_b, chirp, fwd, inv, obuf,
    sem_v, sem_w, sem_ha, sem_hb, sa_send, sa_recv, sa_own, sb_send, sb_recv, sb_own, sem_o,
):
    sec = lax.axis_index("section")
    me = lax.axis_index("grp")
    y, z, x, c = me // (NZ * NX * NC), (me // (NX * NC)) % NZ, (me // NC) % NX, me % NC

    def partner(o):
        dy, dz, dx, dc = o
        return (((y + dy) % NY * NZ + (z + dz) % NZ) * NX + (x + dx) % NX) * NC + (c + dc) % NC

    barrier = pltpu.get_barrier_semaphore()
    for o in ORDER:
        pl.semaphore_signal(barrier, inc=1, device_id=(sec, partner(o)), device_id_type=MESH)
    pl.semaphore_signal(barrier, inc=1, device_id=(1 - sec, me), device_id_type=MESH)

    def load_v(i):
        t = CHUNKS - 1 - i
        return pltpu.make_async_copy(
            volt.at[:, pl.ds(pl.multiple_of(t * (SC * FRAME) - LEAD, 128), SC * FRAME + LEAD)],
            vbuf.at[lax.rem(i, 2)],
            sem_v.at[lax.rem(i, 2)],
        )

    def load_v0():
        return pltpu.make_async_copy(
            volt.at[:, pl.ds(0, SC * FRAME)],
            vbuf.at[(CHUNKS - 1) % 2, :, pl.ds(LEAD, SC * FRAME)],
            sem_v.at[(CHUNKS - 1) % 2],
        )

    def load_w(k):
        return pltpu.make_async_copy(
            weights.at[k // 2, lax.rem(k, 2)], wstage.at[lax.rem(k, 2)], sem_w.at[lax.rem(k, 2)]
        )

    load_v(0).start()
    load_w(0).start()

    row = lax.broadcasted_iota(jnp.int32, (256, 256), 0)
    col = lax.broadcasted_iota(jnp.int32, (256, 256), 1)
    perm[...] = jnp.where((row % 16) * 16 + row // 16 == col, 1.0, 0.0).astype(BF16)

    pl.semaphore_wait(barrier, NG)

    halo_copy = pltpu.make_async_remote_copy(
        volt.at[:, pl.ds(CHUNKS * SC * FRAME - LEAD, LEAD)],
        halo_a,
        sem_ha.at[0],
        sem_ha.at[1],
        device_id=(1 - sec, me),
        device_id_type=MESH,
    )

    @pl.when(sec == 0)
    def _():
        halo_copy.start()
        halo_a[...] = jnp.zeros_like(halo_a)
        recv_b[0] = jnp.zeros((2, ROWS, SC), BF16)

    def channelise(i, carry):
        t = CHUNKS - 1 - i
        slot = lax.rem(i, 2)

        @pl.when(i < CHUNKS - 2)
        def _():
            load_v(i + 1).start()

        @pl.when(i == CHUNKS - 2)
        def _():
            load_v0().start()

        @pl.when(i < CHUNKS - 1)
        def _():
            load_v(i).wait()

        @pl.when(i == CHUNKS - 1)
        def _():
            load_v0().wait()

            @pl.when(sec == 1)
            def _():
                halo_copy.wait_recv()

            vbuf[(CHUNKS - 1) % 2, :, pl.ds(0, LEAD)] = halo_a[...]

        def fir(sb, carry):
            base = pl.multiple_of(sb * (16 * FRAME), 16 * FRAME)
            for q in range(2):
                for s0 in (0, 8):
                    parts = []
                    for p0 in (q * 128, q * 128 + HALF):
                        frames = [
                            vbuf[slot, :, pl.ds(base + (s0 + f) * FRAME + p0, 128)].astype(F32)
                            for f in range(8 + TAPS - 1)
                        ]
                        tap = [taps[pl.ds(k, 1), pl.ds(p0, 128)] for k in range(TAPS)]
                        sums = []
                        for s in range(8):
                            acc = tap[0] * frames[s]
                            for k in range(1, TAPS):
                                acc = acc + tap[k] * frames[s + k]
                            sums.append(acc)
                        parts.append(sums)
                    for s in range(8):
                        lo, hi = parts[0][s], parts[1][s]
                        r0 = (s0 + s) * ANT
                        wblk[pl.ds(r0, ANT), pl.ds(q * 128, 128)] = (lo + hi).astype(BF16)
                        wblk[pl.ds(r0, ANT), pl.ds(HALF + q * 128, 128)] = (lo - hi).astype(BF16)
            moved = jnp.dot(perm[...], wblk[...], preferred_element_type=F32)
            wrow[:, pl.ds(pl.multiple_of(sb * 16, 16), 16), :] = moved.reshape(ANT, 16, FRAME).astype(BF16)
            return carry

        lax.fori_loop(0, SC // 16, fir, 0)

        def dft(ap, carry):
            rows = wrow[pl.ds(ap * 2, 2)].reshape(2 * SC, FRAME)
            for odd in range(2):
                res = lax.dot_general(
                    chan_tab[pl.ds(odd * 256, 256), :],
                    rows[:, odd * HALF : (odd + 1) * HALF],
                    (((1,), (1,)), ((), ())),
                    preferred_element_type=F32,
                ).astype(BF16)
                chan[odd, ap * 2] = res[:, :SC]
                chan[odd, ap * 2 + 1] = res[:, SC:]
            return carry

        lax.fori_loop(0, ANT // 2, dft, 0)

        def regroup(jh, carry):
            js = pl.ds(pl.multiple_of(jh * 16, 16), 16)
            both = jnp.concatenate(
                [chan[0, :, js, :].reshape(256, SC), chan[1, :, js, :].reshape(256, SC)], axis=1
            )
            moved = jnp.dot(perm[...], both, preferred_element_type=F32).astype(BF16)
            send_a[t, pl.ds(jh * 4, 4), pl.ds(0, 4)] = moved[:, :SC].reshape(4, 4, ANT, SC)
            send_a[t, pl.ds(jh * 4, 4), pl.ds(4, 4)] = moved[:, SC:].reshape(4, 4, ANT, SC)
            return carry

        lax.fori_loop(0, 16, regroup, 0)

        mine = pl.ds(pl.multiple_of(me * ANT, ANT), ANT)
        for o in ORDER:
            to = partner(o)
            pltpu.make_async_remote_copy(
                send_a.at[t, to],
                recv_a.at[t, :, mine, :],
                sa_send.at[t],
                sa_recv.at[t],
                device_id=(sec, to),
                device_id_type=MESH,
            ).start()
        pltpu.make_async_copy(send_a.at[t, me], recv_a.at[t, :, mine, :], sa_own.at[t]).start()
        return carry

    lax.fori_loop(0, CHUNKS, channelise, 0)

    def build_onehot(k, carry):
        r0 = pl.multiple_of(k * 128, 128)
        antenna = lax.broadcasted_iota(jnp.int32, (128, ALL_ANT), 0) + r0
        onehot[pl.ds(r0, 128), :] = jnp.where(antenna == ant_row[...], 1.0, 0.0).astype(BF16)
        return carry

    lax.fori_loop(0, ALL_ANT // 128, build_onehot, 0)

    def permute_weights(k, carry):
        @pl.when(k < 2 * CPD - 1)
        def _():
            load_w(k + 1).start()

        load_w(k).wait()

        def tile(n, carry):
            cols = pl.ds(pl.multiple_of(n * 256, 256), 256)
            wperm[k, :, cols] = jnp.dot(
                wstage[lax.rem(k, 2)], onehot[:, cols], preferred_element_type=F32
            ).astype(BF16)
            return carry

        lax.fori_loop(0, ALL_ANT // 256, tile, 0)
        return carry

    lax.fori_loop(0, 2 * CPD, permute_weights, 0)

    cos_t, sin_t = blk_tab[0], blk_tab[1]
    for h in range(2):
        part = slice(h * SC, (h + 1) * SC)
        fwd[pl.ds(h * 2 * SC, SC), pl.ds(0, 256)] = cos_t[part, :]
        fwd[pl.ds(h * 2 * SC, SC), pl.ds(256, 256)] = -sin_t[part, :]
        fwd[pl.ds(h * 2 * SC + SC, SC), pl.ds(0, 256)] = sin_t[part, :]
        fwd[pl.ds(h * 2 * SC + SC, SC), pl.ds(256, 256)] = cos_t[part, :]
    inv[pl.ds(0, 256), pl.ds(0, SC)] = cos_t[:, SC:]
    inv[pl.ds(0, 256), pl.ds(SC, SC)] = sin_t[:, SC:]
    inv[pl.ds(256, 256), pl.ds(0, SC)] = -sin_t[:, SC:]
    inv[pl.ds(256, 256), pl.ds(SC, SC)] = cos_t[:, SC:]

    def build_chirp(k, carry):
        r0 = pl.multiple_of(k * 64, 64)
        rows = lax.broadcasted_iota(jnp.int32, (64, 256), 0) + r0
        channel = (rows // BPD).astype(F32)
        stretch = 1.0 + channel / CH
        strength = 1.0 / (stretch * stretch * stretch)
        dl = jnp.concatenate([delay[...]] * 8, axis=0)
        dl = jnp.concatenate([dl, dl], axis=1)
        f = lax.broadcasted_iota(jnp.int32, (64, 256), 1)
        u = jnp.where(f < SC, f, f - 2 * SC).astype(F32)
        quarters = dl * strength * (u * u) * (1.0 / 32768.0)
        whole = jnp.round(quarters)
        a = (quarters - whole) * (math.pi / 2)
        k4 = (whole.astype(jnp.int32) - f) & 3
        a2 = a * a
        sin_a = a * (1.0 + a2 * (-1.0 / 6 + a2 * (1.0 / 120 + a2 * (-1.0 / 5040 + a2 * (1.0 / 362880)))))
        cos_a = 1.0 + a2 * (
            -0.5 + a2 * (1.0 / 24 + a2 * (-1.0 / 720 + a2 * (1.0 / 40320 + a2 * (-1.0 / 3628800))))
        )
        swap = (k4 & 1) == 1
        cos_p = jnp.where(swap, sin_a, cos_a)
        sin_p = jnp.where(swap, cos_a, sin_a)
        chirp[0, pl.ds(r0, 64), :] = jnp.where((k4 == 1) | (k4 == 2), -cos_p, cos_p)
        chirp[1, pl.ds(r0, 64), :] = jnp.where(k4 >= 2, -sin_p, sin_p)
        return carry

    lax.fori_loop(0, ROWS // 64, build_chirp, 0)

    def form(i, carry):
        t = CHUNKS - 1 - i
        own_rows = pl.ds(pl.multiple_of(me * ANT, ANT), ANT)
        got = recv_a.at[t, :, pl.ds(0, (NG - 1) * ANT), :]
        pltpu.make_async_remote_copy(
            got, got, sa_send.at[t], sa_recv.at[t], device_id=(sec, me), device_id_type=MESH
        ).wait_recv()
        pltpu.make_async_copy(send_a.at[t, me], recv_a.at[t, :, own_rows, :], sa_own.at[t]).wait()

        def pair(cp, carry):
            for cc in range(2):
                both = jnp.concatenate(
                    [recv_a[t, cc * 4 + cp * 2], recv_a[t, cc * 4 + cp * 2 + 1]], axis=1
                )
                w = cp * 4 + cc * 2
                for h in range(2):
                    bs = pl.ds(h * 256, 256)
                    by_real = jnp.dot(wperm[w, bs, :], both, preferred_element_type=F32)
                    by_imag = jnp.dot(wperm[w + 1, bs, :], both, preferred_element_type=F32)
                    btmp[cc, 0, bs, :] = by_real[:, :SC] - by_imag[:, SC:]
                    btmp[cc, 1, bs, :] = by_real[:, SC:] + by_imag[:, :SC]
            rs = pl.ds(pl.multiple_of(cp * 16, 16), 16)
            for ri in range(2):
                for h in range(4):
                    ds = pl.ds(h * 16, 16)
                    joined = jnp.concatenate(
                        [btmp[cc, ri, pl.ds(h * 128, 128), :].reshape(16, BPD, SC) for cc in range(2)],
                        axis=1,
                    )
                    send_b[t, ri, ds, rs, :] = joined.astype(BF16)
            return carry

        lax.fori_loop(0, CPD // 2, pair, 0)

        mine = pl.ds(pl.multiple_of(me * (CPD * BPD), CPD * BPD), CPD * BPD)
        for o in ORDER:
            to = partner(o)
            pltpu.make_async_remote_copy(
                send_b.at[t, :, to],
                recv_b.at[t + 1, :, mine, :],
                sb_send.at[t],
                sb_recv.at[t],
                device_id=(sec, to),
                device_id_type=MESH,
            ).start()
        pltpu.make_async_copy(send_b.at[t, :, me], recv_b.at[t + 1, :, mine, :], sb_own.at[t]).start()
        return carry

    lax.fori_loop(0, CHUNKS, form, 0)

    def wait_series(t):
        mine = pl.ds(pl.multiple_of(me * (CPD * BPD), CPD * BPD), CPD * BPD)
        got = recv_b.at[t + 1, :, pl.ds(0, (NG - 1) * CPD * BPD), :]
        pltpu.make_async_remote_copy(
            got, got, sb_send.at[t], sb_recv.at[t], device_id=(sec, me), device_id_type=MESH
        ).wait_recv()
        pltpu.make_async_copy(send_b.at[t, :, me], recv_b.at[t + 1, :, mine, :], sb_own.at[t]).wait()

    wait_series(CHUNKS - 1)
    halo_b = pltpu.make_async_remote_copy(
        recv_b.at[CHUNKS],
        recv_b.at[0],
        sem_hb.at[0],
        sem_hb.at[1],
        device_id=(1 - sec, me),
        device_id_type=MESH,
    )

    @pl.when(sec == 0)
    def _():
        halo_b.start()

    def store_out(m):
        return pltpu.make_async_copy(
            obuf.at[lax.rem(m, 2)],
            out.at[:, :, :, pl.ds(pl.multiple_of(m * SC, SC), SC)],
            sem_o.at[lax.rem(m, 2)],
        )

    def dedisperse(i, carry):
        m = CHUNKS - 1 - i

        @pl.when(m > 0)
        def _():
            wait_series(m - 1)

        @pl.when((m == 0) & (sec == 1))
        def _():
            halo_b.wait_recv()

        @pl.when(i >= 2)
        def _():
            store_out(m + 2).wait()

        def tile(r, carry):
            rs = pl.ds(pl.multiple_of(r * RT, RT), RT)
            block = jnp.concatenate(
                [recv_b[m, 0, rs, :], recv_b[m, 1, rs, :], recv_b[m + 1, 0, rs, :], recv_b[m + 1, 1, rs, :]],
                axis=1,
            )
            spec = jnp.dot(block, fwd[...], preferred_element_type=F32)
            sr, si = spec[:, :256], spec[:, 256:]
            cr, ci = chirp[0, rs, :], chirp[1, rs, :]
            filtered = jnp.concatenate(
                [(sr * cr - si * ci).astype(BF16), (sr * ci + si * cr).astype(BF16)], axis=1
            )
            res = jnp.dot(filtered, inv[...], preferred_element_type=F32)
            cs = pl.ds(pl.multiple_of(r * (RT // BPD), RT // BPD), RT // BPD)
            obuf[lax.rem(m, 2), cs, 0] = res[:, :SC].reshape(RT // BPD, BPD, SC)
            obuf[lax.rem(m, 2), cs, 1] = res[:, SC:].reshape(RT // BPD, BPD, SC)
            return carry

        lax.fori_loop(0, ROWS // RT, tile, 0)
        store_out(m).start()
        return carry

    lax.fori_loop(0, CHUNKS, dedisperse, 0)

    store_out(1).wait()
    store_out(0).wait()

    @pl.when(sec == 0)
    def _():
        halo_copy.wait_send()
        halo_b.wait_send()

    for t in range(CHUNKS):
        sent = send_a.at[t, pl.ds(0, NG - 1)]
        pltpu.make_async_remote_copy(
            sent, sent, sa_send.at[t], sa_recv.at[t], device_id=(sec, me), device_id_type=MESH
        ).wait_send()
        sent = send_b.at[t, :, pl.ds(0, NG - 1)]
        pltpu.make_async_remote_copy(
            sent, sent, sb_send.at[t], sb_recv.at[t], device_id=(sec, me), device_id_type=MESH
        ).wait_send()


def local(voltages, filter_taps, beam_weights, antenna_of_row, beam_delay):
    chan_tab = jnp.asarray(channel_tables()).astype(BF16)
    blk_tab = jnp.asarray(block_tables()).astype(BF16)
    ant_row = antenna_of_row.reshape(1, ALL_ANT)
    delay = jnp.broadcast_to(beam_delay.astype(F32)[:, None], (BPD, 128))
    vmem = pl.BlockSpec(memory_space=pltpu.VMEM)
    hbm = pl.BlockSpec(memory_space=pl.ANY)
    dma = pltpu.SemaphoreType.DMA
    return pl.pallas_call(
        kernel,
        out_shape=jax.ShapeDtypeStruct((CH, 2, BPD, CHUNKS * SC), F32),
        in_specs=[hbm, vmem, hbm, vmem, vmem, vmem, vmem],
        out_specs=hbm,
        scratch_shapes=[
            pltpu.VMEM((2, ANT, SC * FRAME + LEAD), BF16),
            pltpu.VMEM((ANT, LEAD), BF16),
            pltpu.VMEM((256, FRAME), BF16),
            pltpu.VMEM((ANT, SC, FRAME), BF16),
            pltpu.VMEM((2, ANT, 256, SC), BF16),
            pltpu.VMEM((CHUNKS, NG, 2 * CPD, ANT, SC), BF16),
            pltpu.VMEM((CHUNKS, 2 * CPD, ALL_ANT, SC), BF16),
            pltpu.VMEM((256, 256), BF16),
            pltpu.VMEM((ALL_ANT, ALL_ANT), BF16),
            pltpu.VMEM((2, BEAMS, ALL_ANT), BF16),
            pltpu.VMEM((2 * CPD, BEAMS, ALL_ANT), BF16),
            pltpu.VMEM((2, 2, BEAMS, SC), F32),
            pltpu.VMEM((CHUNKS, 2, NG, CPD * BPD, SC), BF16),
            pltpu.VMEM((CHUNKS + 1, 2, ROWS, SC), BF16),
            pltpu.VMEM((2, ROWS, 256), F32),
            pltpu.VMEM((512, 512), BF16),
            pltpu.VMEM((512, 256), BF16),
            pltpu.VMEM((2, CH, 2, BPD, SC), F32),
            dma((2,)), dma((2,)), dma((2,)), dma((2,)),
            dma((CHUNKS,)), dma((CHUNKS,)), dma((CHUNKS,)),
            dma((CHUNKS,)), dma((CHUNKS,)), dma((CHUNKS,)),
            dma((2,)),
        ],
        compiler_params=pltpu.CompilerParams(
            collective_id=0, has_side_effects=True, vmem_limit_bytes=67043328
        ),
    )(voltages, filter_taps, beam_weights, ant_row, delay, chan_tab, blk_tab)


def solution(mesh):
    in_specs = (P("grp", "section"), P(), P("grp", None, None, None), P(), P("grp"))
    out_specs = P(None, None, "grp", "section")
    return jax.shard_map(local, mesh=mesh, in_specs=in_specs, out_specs=out_specs, check_vma=False)
```

time: 436 us -> 194 us (0.44)
  the two profiles are of different devices: /device:TPU:70 before, /device:TPU:4 now
where the time goes in v1:
time: 194 us
  Pallas kernels  184 us (95%)
  local copies, waits for them, and re-layouts  9.36 us (5%)
    pallas_call x1, Pallas kernels, local(): pl.pallas_call(kernel, out_shape=jax.ShapeDtypeStruct((CH, 2, BPD, CHUNKS...  184 us
    unnamed x1, local copies, waits for them, and re-layouts  8.7 us

profile of v1, /device:TPU:4, one launch (start us, length us, event | category | flops | bytes accessed | tf_op | source)
XLA Modules:
  0.0 194.1 jit_solution(5078907542623893570)
XLA Ops:
  0.0 0.7 convert_element_type.9
  0.7 0.7 broadcast_in_dim.2.delay
  1.3 184.0 %shard_map.73 = f32[256,2,8,512]{3,2,1,0:T(8,128)} custom-call(bf16[16,262144]{1,0:T(8,128)(2,1)} %volt.1, f32[8,512]{1,0:T(8,128)} %taps.1, bf16[4,2,512,1024]{3,2,1,0:T(8,128)(2,1)} %weights.1, s32[1,1024]{1,0:T(1,128)} %bitcast.1, f32[8,128]{1,0:T(8,128)} %broadcast_in_dim.2.delay, bf16[512,256]{1,0:T(8,128)(2,1)} %constant.9.chan_tab, ...), custom_call_target="tpu_custom_call" | custom-call | tf_op jit(solution)/shard_map/pallas_call | solution.py:462
  185.4 8.7 %copy.9 = f32[256,2,8,512]{3,2,1,0:T(8,128)} copy(f32[256,2,8,512]{3,2,1,0:T(8,128)} %shard_map.73) | data formatting | bytes 16777216

commit v2 on v1

v2 whole, which is shorter than its diff:
```python
import functools
import math
import random

import jax
import jax.numpy as jnp
import numpy as np
from jax import lax
from jax.experimental import pallas as pl
from jax.experimental.pallas import tpu as pltpu
from jax.sharding import PartitionSpec as P

MESH = pl.DeviceIdType.MESH
F32 = jnp.float32
BF16 = jnp.bfloat16
NG = 64
NY, NZ, NX, NC = 4, 4, 2, 2
ANT = 16
FRAME = 512
HALF = FRAME // 2
TAPS = 8
CH = 256
CPD = CH // NG
CHUNKS = 4
SC = 128
LEAD = (TAPS - 1) * FRAME
BEAMS = 512
BPD = BEAMS // NG
ROWS = CH * BPD
ALL_ANT = ANT * NG
HROWS = ROWS // 2
RT = 256
VMEM_LIMIT = 55 * 2**20


def send_order(seed=0):
    rng = random.Random(seed)
    left = [
        (dy, dz, dx, dc) for dy in range(NY) for dz in range(NZ) for dx in range(NX) for dc in range(NC)
    ][1:]
    rng.shuffle(left)
    load = {}

    def ports(o):
        p = []
        for name, d in (("y", o[0]), ("z", o[1])):
            if d in (1, 2):
                p.append(name + "+")
            if d in (2, 3):
                p.append(name + "-")
        if o[2]:
            p.append("x")
        return p

    out = []
    while left:
        best = min(
            left,
            key=lambda o: (max([load.get(p, 0) + 1 for p in ports(o)] + [0]), -len(ports(o)), rng.random()),
        )
        for p in ports(best):
            load[p] = load.get(p, 0) + 1
        out.append(best)
        left.remove(best)
    return out


ORDER = send_order()
CROSS = [o for o in ORDER if o[2]]


def channel_tables():
    j = np.arange(256)
    p = np.arange(HALF)
    tables = []
    for odd in (0, 1):
        channel = (j // 4) * CPD + ((j // 2) % 2) * 2 + odd
        angle = 2.0 * np.pi * ((channel[:, None] * p[None, :]) % FRAME) / FRAME
        value = np.where((j % 2)[:, None] == 0, np.cos(angle), -np.sin(angle)) / math.sqrt(CH)
        tables.append(value.astype(np.float32))
    return np.concatenate(tables, axis=0)


def block_tables():
    n = np.arange(2 * SC)
    angle = 2.0 * np.pi * ((n[:, None] * n[None, :]) % (2 * SC)) / (2 * SC)
    factor = 1.0 / math.sqrt(2 * SC)
    return np.stack([np.cos(angle) * factor, np.sin(angle) * factor]).astype(np.float32)


def kernel(
    volt, taps_h, weights, ant_row_h, delay, chan_tab_h, blk_tab_h,
    out,
    vbuf, halo_a, wblk, wrow, chan, send_a, recv_a, perm, onehot, wstage, wperm,
    btmp, send_b, recv_b, relay, chirp, fwd, inv, taps, ant_row, chan_tab, blk_tab,
    sem_v, sem_w, sem_t, sem_ha, sem_hb, sem_rl, sem_fw, sem_mc, sa_send, sa_recv, sb_send, sb_recv,
):
    sec = lax.axis_index("section")
    me = lax.axis_index("grp")
    y, z, x, c = me // (NZ * NX * NC), (me // (NX * NC)) % NZ, (me // NC) % NX, me % NC

    def partner(o):
        dy, dz, dx, dc = o
        return (((y + dy) % NY * NZ + (z + dz) % NZ) * NX + (x + dx) % NX) * NC + (c + dc) % NC

    def load_v(i):
        t = CHUNKS - 1 - i
        return pltpu.make_async_copy(
            volt.at[:, pl.ds(pl.multiple_of(t * (SC * FRAME) - LEAD, 128), SC * FRAME + LEAD)],
            vbuf.at[lax.rem(i, 2)],
            sem_v.at[lax.rem(i, 2)],
        )

    def load_v0():
        return pltpu.make_async_copy(
            volt.at[:, pl.ds(0, SC * FRAME)],
            vbuf.at[(CHUNKS - 1) % 2, :, pl.ds(LEAD, SC * FRAME)],
            sem_v.at[(CHUNKS - 1) % 2],
        )

    def load_w(k):
        return pltpu.make_async_copy(
            weights.at[k // 2, lax.rem(k, 2)], wstage.at[lax.rem(k, 2)], sem_w.at[lax.rem(k, 2)]
        )

    small = [
        pltpu.make_async_copy(src, dst, sem_t.at[n])
        for n, (src, dst) in enumerate(
            ((taps_h, taps), (chan_tab_h, chan_tab), (ant_row_h, ant_row), (blk_tab_h, blk_tab))
        )
    ]

    load_v(0).start()
    for copy in small:
        copy.start()
    load_w(0).start()
    barrier = pltpu.get_barrier_semaphore()
    for o in ORDER:
        pl.semaphore_signal(barrier, inc=1, device_id=(sec, partner(o)), device_id_type=MESH)
    for o in CROSS:
        pl.semaphore_signal(barrier, inc=1, device_id=(1 - sec, partner(o)), device_id_type=MESH)
    pl.semaphore_signal(barrier, inc=1, device_id=(1 - sec, me), device_id_type=MESH)

    row = lax.broadcasted_iota(jnp.int32, (256, 256), 0)
    col = lax.broadcasted_iota(jnp.int32, (256, 256), 1)
    perm[...] = jnp.where((row % 16) * 16 + row // 16 == col, 1.0, 0.0).astype(BF16)
    wblk[...] = jnp.zeros_like(wblk)
    small[0].wait()
    small[1].wait()

    halo_copy = pltpu.make_async_remote_copy(
        volt.at[:, pl.ds(CHUNKS * SC * FRAME - LEAD, LEAD)],
        halo_a,
        sem_ha.at[0],
        sem_ha.at[1],
        device_id=(1 - sec, me),
        device_id_type=MESH,
    )

    def fir_block(slot, sb, wslot):
        base = pl.multiple_of(sb * (16 * FRAME), 16 * FRAME)
        for q in range(2):
            for s0 in (0, 8):
                parts = []
                for p0 in (q * 128, q * 128 + HALF):
                    frames = [
                        vbuf[slot, :, pl.ds(base + (s0 + f) * FRAME + p0, 128)].astype(F32)
                        for f in range(8 + TAPS - 1)
                    ]
                    tap = [taps[pl.ds(k, 1), pl.ds(p0, 128)] for k in range(TAPS)]
                    sums = []
                    for s in range(8):
                        acc = tap[0] * frames[s]
                        for k in range(1, TAPS):
                            acc = acc + tap[k] * frames[s + k]
                        sums.append(acc)
                    parts.append(sums)
                for s in range(8):
                    lo, hi = parts[0][s], parts[1][s]
                    r0 = (s0 + s) * ANT
                    wblk[wslot, pl.ds(r0, ANT), pl.ds(q * 128, 128)] = (lo + hi).astype(BF16)
                    wblk[wslot, pl.ds(r0, ANT), pl.ds(HALF + q * 128, 128)] = (lo - hi).astype(BF16)

    def move_rows(wslot):
        return jnp.dot(perm[...], wblk[wslot], preferred_element_type=F32).reshape(ANT, 16, FRAME).astype(BF16)

    def channelise(i, carry):
        t = CHUNKS - 1 - i
        slot = lax.rem(i, 2)

        @pl.when(i < CHUNKS - 2)
        def _():
            load_v(i + 1).start()

        @pl.when(i == CHUNKS - 2)
        def _():
            load_v0().start()

        @pl.when(i < CHUNKS - 1)
        def _():
            load_v(i).wait()

        @pl.when(i == CHUNKS - 1)
        def _():
            load_v0().wait()

            @pl.when(sec == 1)
            def _():
                halo_copy.wait_recv()

            vbuf[(CHUNKS - 1) % 2, :, pl.ds(0, LEAD)] = halo_a[...]

        def fir(sb, carry):
            moved = move_rows(lax.rem(sb + 1, 2))
            fir_block(slot, sb, lax.rem(sb, 2))
            before = pl.multiple_of(jnp.maximum(sb - 1, 0) * 16, 16)
            wrow[:, pl.ds(before, 16), :] = moved
            return carry

        nblk = SC // 16
        lax.fori_loop(0, nblk, fir, 0)
        wrow[:, pl.ds((nblk - 1) * 16, 16), :] = move_rows((nblk - 1) % 2)

        def dft(ap2, carry):
            for u in range(2):
                ap = ap2 * 2 + u
                rows = wrow[pl.ds(ap * 2, 2)].reshape(2 * SC, FRAME)
                for odd in range(2):
                    res = lax.dot_general(
                        chan_tab[pl.ds(odd * 256, 256), :],
                        rows[:, odd * HALF : (odd + 1) * HALF],
                        (((1,), (1,)), ((), ())),
                        preferred_element_type=F32,
                    ).astype(BF16)
                    chan[odd, ap * 2] = res[:, :SC]
                    chan[odd, ap * 2 + 1] = res[:, SC:]
            return carry

        lax.fori_loop(0, ANT // 4, dft, 0)

        @pl.when(i == 0)
        def _():
            pl.semaphore_wait(barrier, NG + NG // 2)

        mine = pl.ds(pl.multiple_of(me * ANT, ANT), ANT)

        def shift(s):
            return s % NY, (s // NY + s % NY) % NZ

        def regroup(s):
            dy, dz = shift(s)
            jh = (y + dy) % NY * NZ + (z + dz) % NZ
            js = pl.ds(pl.multiple_of(jh * 16, 16), 16)
            both = jnp.concatenate(
                [chan[0, :, js, :].reshape(256, SC), chan[1, :, js, :].reshape(256, SC)], axis=1
            )
            moved = jnp.dot(perm[...], both, preferred_element_type=F32).astype(BF16)
            send_a[t, pl.ds(jh * 4, 4), pl.ds(0, 4)] = moved[:, :SC].reshape(4, 4, ANT, SC)
            send_a[t, pl.ds(jh * 4, 4), pl.ds(4, 4)] = moved[:, SC:].reshape(4, 4, ANT, SC)

        def send(s, pairs):
            dy, dz = shift(s)
            for dx, dc in pairs:
                to = partner((dy, dz, dx, dc))
                pltpu.make_async_remote_copy(
                    send_a.at[t, to],
                    recv_a.at[t, :, mine, :],
                    sa_send.at[t],
                    sa_recv.at[t],
                    device_id=(sec, to),
                    device_id_type=MESH,
                ).start()

        nshift = NY * NZ
        regroup(1)

        def step(k, carry):
            regroup(lax.rem(k + 2, nshift))
            send(k + 1, ((1, 0), (0, 1), (1, 1), (0, 0)))
            return carry

        lax.fori_loop(0, nshift - 1, step, 0)
        send(0, ((1, 0), (0, 1), (1, 1)))
        pltpu.make_async_copy(send_a.at[t, me], recv_a.at[t, :, mine, :], sa_recv.at[t]).start()

        @pl.when((i == 0) & (sec == 0))
        def _():
            halo_copy.start()
            halo_a[...] = jnp.zeros_like(halo_a)
            recv_b[0] = jnp.zeros((2, 2, NY * NZ, NX, 32, SC), BF16)

        return carry

    lax.fori_loop(0, CHUNKS - 1, channelise, 0)

    small[2].wait()

    def build_onehot(k, carry):
        r0 = pl.multiple_of(k * 128, 128)
        antenna = lax.broadcasted_iota(jnp.int32, (128, ALL_ANT), 0) + r0
        onehot[pl.ds(r0, 128), :] = jnp.where(antenna == ant_row[...], 1.0, 0.0).astype(BF16)
        return carry

    lax.fori_loop(0, ALL_ANT // 128, build_onehot, 0)

    def permute_weights(k, carry):
        @pl.when(k < 2 * CPD - 1)
        def _():
            load_w(k + 1).start()

        load_w(k).wait()

        def tile(n, carry):
            cols = pl.ds(pl.multiple_of(n * 256, 256), 256)
            wperm[k, :, cols] = jnp.dot(
                wstage[lax.rem(k, 2)], onehot[:, cols], preferred_element_type=F32
            ).astype(BF16)
            return carry

        lax.fori_loop(0, ALL_ANT // 256, tile, 0)
        return carry

    lax.fori_loop(0, 2 * CPD, permute_weights, 0)

    small[3].wait()
    cos_t, sin_t = blk_tab[0], blk_tab[1]
    for h in range(2):
        part = slice(h * SC, (h + 1) * SC)
        fwd[pl.ds(h * 2 * SC, SC), pl.ds(0, 256)] = cos_t[part, :]
        fwd[pl.ds(h * 2 * SC, SC), pl.ds(256, 256)] = -sin_t[part, :]
        fwd[pl.ds(h * 2 * SC + SC, SC), pl.ds(0, 256)] = sin_t[part, :]
        fwd[pl.ds(h * 2 * SC + SC, SC), pl.ds(256, 256)] = cos_t[part, :]
    inv[pl.ds(0, 256), pl.ds(0, SC)] = cos_t[:, SC:]
    inv[pl.ds(0, 256), pl.ds(SC, SC)] = sin_t[:, SC:]
    inv[pl.ds(256, 256), pl.ds(0, SC)] = -sin_t[:, SC:]
    inv[pl.ds(256, 256), pl.ds(SC, SC)] = cos_t[:, SC:]

    beam = lax.broadcasted_iota(jnp.int32, (BPD, 256), 0)
    dl8 = jnp.zeros((BPD, 256), F32)
    for b in range(BPD):
        dl8 = jnp.where(beam == b, delay[b].astype(F32), dl8)
    dl = jnp.concatenate([dl8] * 8, axis=0)

    def build_chirp(k, carry):
        half, r0 = k // (HROWS // 64), pl.multiple_of(lax.rem(k, HROWS // 64) * 64, 64)
        rows = lax.broadcasted_iota(jnp.int32, (64, 256), 0) + r0
        channel = (rows // 16 * CPD + half * 2 + (rows // BPD) % 2).astype(F32)
        stretch = 1.0 + channel / CH
        strength = 1.0 / (stretch * stretch * stretch)
        f = lax.broadcasted_iota(jnp.int32, (64, 256), 1)
        u = jnp.where(f < SC, f, f - 2 * SC).astype(F32)
        quarters = dl * strength * (u * u) * (1.0 / 32768.0)
        whole = jnp.round(quarters)
        a = (quarters - whole) * (math.pi / 2)
        k4 = (whole.astype(jnp.int32) - f) & 3
        a2 = a * a
        sin_a = a * (1.0 + a2 * (-1.0 / 6 + a2 * (1.0 / 120 + a2 * (-1.0 / 5040 + a2 * (1.0 / 362880)))))
        cos_a = 1.0 + a2 * (
            -0.5 + a2 * (1.0 / 24 + a2 * (-1.0 / 720 + a2 * (1.0 / 40320 + a2 * (-1.0 / 3628800))))
        )
        swap = (k4 & 1) == 1
        cos_p = jnp.where(swap, sin_a, cos_a)
        sin_p = jnp.where(swap, cos_a, sin_a)
        chirp[0, half, pl.ds(r0, 64), :] = jnp.where((k4 == 1) | (k4 == 2), -cos_p, cos_p)
        chirp[1, half, pl.ds(r0, 64), :] = jnp.where(k4 >= 2, -sin_p, sin_p)
        return carry

    lax.fori_loop(0, ROWS // 64, build_chirp, 0)

    own_b = pl.ds(pl.multiple_of(c * 16, 16), 16)
    yz = me // (NX * NC)

    def form(i, carry):
        t = CHUNKS - 1 - i
        got = recv_a.at[t]
        pltpu.make_async_remote_copy(
            got, got, sa_send.at[t], sa_recv.at[t], device_id=(sec, me), device_id_type=MESH
        ).wait_recv()

        def pair(cp, carry):
            for cc in range(2):
                both = jnp.concatenate(
                    [recv_a[t, cc * 4 + cp * 2], recv_a[t, cc * 4 + cp * 2 + 1]], axis=1
                )
                w = cp * 4 + cc * 2
                for h in range(2):
                    bs = pl.ds(h * 256, 256)
                    by_real = jnp.dot(wperm[w, bs, :], both, preferred_element_type=F32)
                    by_imag = jnp.dot(wperm[w + 1, bs, :], both, preferred_element_type=F32)
                    btmp[cc, 0, bs, :] = by_real[:, :SC] - by_imag[:, SC:]
                    btmp[cc, 1, bs, :] = by_real[:, SC:] + by_imag[:, :SC]
            for ri in range(2):
                for h in range(4):
                    joined = jnp.concatenate(
                        [btmp[cc, ri, pl.ds(h * 128, 128), :].reshape(16, BPD, SC) for cc in range(2)],
                        axis=1,
                    )
                    send_b[t, cp, ri, pl.ds(h * 16, 16)] = joined.astype(BF16)
            pltpu.make_async_copy(
                send_b.at[t, cp, :, me], recv_b.at[t + 1, cp, :, yz, x, own_b, :], sb_recv.at[t, cp]
            ).start()
            for o in ORDER:
                to = partner(o)
                pltpu.make_async_remote_copy(
                    send_b.at[t, cp, :, to],
                    recv_b.at[t + 1, cp, :, yz, x, own_b, :],
                    sb_send.at[t, cp],
                    sb_recv.at[t, cp],
                    device_id=(sec, to),
                    device_id_type=MESH,
                ).start()

            @pl.when((i == 0) & (sec == 0))
            def _():
                for o in CROSS:
                    to = partner(o)
                    pltpu.make_async_remote_copy(
                        send_b.at[CHUNKS - 1, cp, :, to],
                        recv_b.at[0, cp, :, yz, x, own_b, :],
                        sem_mc.at[0, cp],
                        sem_mc.at[1, cp],
                        device_id=(1 - sec, to),
                        device_id_type=MESH,
                    ).start()

            return carry

        lax.fori_loop(0, 2, pair, 0)
        return carry

    lax.fori_loop(0, 1, form, 0)
    lax.fori_loop(CHUNKS - 1, CHUNKS, channelise, 0)
    lax.fori_loop(1, CHUNKS - 1, form, 0)

    def wait_series(t, cp):
        got = recv_b.at[t + 1, cp]
        pltpu.make_async_remote_copy(
            got, got, sb_send.at[t, cp], sb_recv.at[t, cp], device_id=(sec, me), device_id_type=MESH
        ).wait_recv()

    flip = partner((0, 0, 1, 0))
    wait_series(CHUNKS - 1, 0)
    wait_series(CHUNKS - 1, 1)
    halo_b = pltpu.make_async_remote_copy(
        recv_b.at[CHUNKS, 0, :, :, x],
        recv_b.at[0, 0, :, :, x],
        sem_hb.at[0],
        sem_hb.at[1],
        device_id=(1 - sec, me),
        device_id_type=MESH,
    )
    to_relay = pltpu.make_async_remote_copy(
        recv_b.at[CHUNKS, 1, :, :, x],
        relay,
        sem_rl.at[0],
        sem_rl.at[1],
        device_id=(1 - sec, flip),
        device_id_type=MESH,
    )
    forward = pltpu.make_async_remote_copy(
        relay,
        recv_b.at[0, 1, :, :, 1 - x],
        sem_fw.at[0],
        sem_fw.at[1],
        device_id=(sec, flip),
        device_id_type=MESH,
    )

    @pl.when(sec == 0)
    def _():
        to_relay.start()
        halo_b.start()

    lax.fori_loop(CHUNKS - 1, CHUNKS, form, 0)

    @pl.when(sec == 1)
    def _():
        to_relay.wait_recv()
        forward.start()

    def dedisperse(n, carry):
        late = n // 4
        m = (1 - late) * (3 - n // 2) + late * (1 - n % 2)
        cp = (1 - late) * (n % 2) + late * ((n // 2) % 2)

        @pl.when(m > 0)
        def _():
            wait_series(m - 1, cp)

        @pl.when((n == 5) & (sec == 1))
        def _():
            halo_b.wait_recv()
            pltpu.make_async_remote_copy(
                relay, recv_b.at[0, 1, :, :, x], sem_fw.at[0], sem_fw.at[1],
                device_id=(sec, flip), device_id_type=MESH,
            ).wait_recv()
            for half in range(2):
                got = recv_b.at[0, half, :, :, 1 - x]
                pltpu.make_async_remote_copy(
                    got, got, sem_mc.at[0, half], sem_mc.at[1, half],
                    device_id=(sec, flip), device_id_type=MESH,
                ).wait_recv()

        def tile(r, carry):
            rs = pl.ds(pl.multiple_of(r * RT, RT), RT)
            qs = pl.ds(r * (RT // 64), RT // 64)
            block = jnp.concatenate(
                [recv_b[m + d, cp, ri, qs].reshape(RT, SC) for d in range(2) for ri in range(2)], axis=1
            )
            spec = jnp.dot(block, fwd[...], preferred_element_type=F32)
            sr, si = spec[:, :256], spec[:, 256:]
            cr, ci = chirp[0, cp, rs, :], chirp[1, cp, rs, :]
            filtered = jnp.concatenate(
                [(sr * cr - si * ci).astype(BF16), (sr * ci + si * cr).astype(BF16)], axis=1
            )
            res = jnp.dot(filtered, inv[...], preferred_element_type=F32)
            gs = pl.ds(r * (RT // 16), RT // 16)
            ns = pl.ds(pl.multiple_of(m * SC, SC), SC)
            for ri in range(2):
                part = res[:, ri * SC : (ri + 1) * SC].reshape(RT // 16, 2, BPD, SC)
                for cc in range(2):
                    out[gs, cp * 2 + cc, ri, :, ns] = part[:, cc]
            return carry

        lax.fori_loop(0, HROWS // RT, tile, 0)
        return carry

    lax.fori_loop(0, 2 * CHUNKS, dedisperse, 0)

    @pl.when(sec == 0)
    def _():
        halo_copy.wait_send()
        halo_b.wait_send()
        to_relay.wait_send()
        for half in range(2):
            sent = send_b.at[CHUNKS - 1, half, :, pl.ds(0, NG // 2)]
            pltpu.make_async_remote_copy(
                sent, sent, sem_mc.at[0, half], sem_mc.at[1, half],
                device_id=(1 - sec, me), device_id_type=MESH,
            ).wait_send()

    @pl.when(sec == 1)
    def _():
        forward.wait_send()

    for t in range(CHUNKS):
        sent = send_a.at[t, pl.ds(0, NG - 1)]
        pltpu.make_async_remote_copy(
            sent, sent, sa_send.at[t], sa_recv.at[t], device_id=(sec, me), device_id_type=MESH
        ).wait_send()
        for cp in range(2):
            sent = send_b.at[t, cp, :, pl.ds(0, NG - 1)]
            pltpu.make_async_remote_copy(
                sent, sent, sb_send.at[t, cp], sb_recv.at[t, cp], device_id=(sec, me), device_id_type=MESH
            ).wait_send()


def local(voltages, filter_taps, beam_weights, antenna_of_row, beam_delay):
    chan_tab = jnp.asarray(channel_tables()).astype(BF16)
    blk_tab = jnp.asarray(block_tables()).astype(BF16)
    ant_row = antenna_of_row.reshape(1, ALL_ANT)
    vmem = pl.BlockSpec(memory_space=pltpu.VMEM)
    smem = pl.BlockSpec(memory_space=pltpu.SMEM)
    hbm = pl.BlockSpec(memory_space=pl.ANY)
    dma = pltpu.SemaphoreType.DMA
    series = pl.pallas_call(
        kernel,
        out_shape=pltpu.VMEM((NG, CPD, 2, BPD, CHUNKS * SC), F32),
        in_specs=[hbm, hbm, hbm, hbm, smem, hbm, hbm],
        out_specs=vmem,
        scratch_shapes=[
            pltpu.VMEM((2, ANT, SC * FRAME + LEAD), BF16),
            pltpu.VMEM((ANT, LEAD), BF16),
            pltpu.VMEM((2, 256, FRAME), BF16),
            pltpu.VMEM((ANT, SC, FRAME), BF16),
            pltpu.VMEM((2, ANT, 256, SC), BF16),
            pltpu.VMEM((CHUNKS, NG, 2 * CPD, ANT, SC), BF16),
            pltpu.VMEM((CHUNKS, 2 * CPD, ALL_ANT, SC), BF16),
            pltpu.VMEM((256, 256), BF16),
            pltpu.VMEM((ALL_ANT, ALL_ANT), BF16),
            pltpu.VMEM((2, BEAMS, ALL_ANT), BF16),
            pltpu.VMEM((2 * CPD, BEAMS, ALL_ANT), BF16),
            pltpu.VMEM((2, 2, BEAMS, SC), F32),
            pltpu.VMEM((CHUNKS, 2, 2, NG, 16, SC), BF16),
            pltpu.VMEM((CHUNKS + 1, 2, 2, NY * NZ, NX, 32, SC), BF16),
            pltpu.VMEM((2, NY * NZ, 32, SC), BF16),
            pltpu.VMEM((2, 2, HROWS, 256), F32),
            pltpu.VMEM((512, 512), BF16),
            pltpu.VMEM((512, 256), BF16),
            pltpu.VMEM((TAPS, FRAME), F32),
            pltpu.VMEM((1, ALL_ANT), jnp.int32),
            pltpu.VMEM((512, HALF), BF16),
            pltpu.VMEM((2, 256, 256), BF16),
            dma((2,)), dma((2,)), dma((4,)), dma((2,)), dma((2,)), dma((2,)), dma((2,)), dma((2, 2)),
            dma((CHUNKS,)), dma((CHUNKS,)), dma((CHUNKS, 2)), dma((CHUNKS, 2)),
        ],
        compiler_params=pltpu.CompilerParams(
            collective_id=0, has_side_effects=True, vmem_limit_bytes=VMEM_LIMIT
        ),
    )(voltages, filter_taps, beam_weights, ant_row, beam_delay, chan_tab, blk_tab)
    return series.reshape(CH, 2, BPD, CHUNKS * SC)


def solution(mesh):
    in_specs = (P("grp", "section"), P(), P("grp", None, None, None), P(), P("grp"))
    out_specs = P(None, None, "grp", "section")
    return jax.shard_map(local, mesh=mesh, in_specs=in_specs, out_specs=out_specs, check_vma=False)
```

time: 194 us -> 171 us (0.88)
  Pallas kernels: 184 us -> 167 us
  local copies, waits for them, and re-layouts: 9.36 us -> 3.4 us
    pallas_call x1, Pallas kernels: 184 us -> 167 us  [local(): pl.pallas_call(kernel, out_shape=pltpu.VMEM((NG, CPD, 2, BPD, CHUNKS * SC...]
    unnamed x1, local copies, waits for them, and re-layouts: 8.7 us -> 3.4 us
where the time goes in v2:
time: 171 us; the launch traced here: 170 us
  Pallas kernels  167 us (98%)
  local copies, waits for them, and re-layouts  3.4 us (2%)
    pallas_call x1, Pallas kernels, local(): pl.pallas_call(kernel, out_shape=pltpu.VMEM((NG, CPD, 2, BPD, CHUNKS * SC...  167 us

profile of v2, /device:TPU:4, one launch (start us, length us, event | category | flops | bytes accessed | tf_op | source)
XLA Modules:
  0.0 170.1 jit_solution(1711040478552466438)
XLA Ops:
  0.0 166.7 %shard_map.73 = f32[64,4,2,8,512]{4,3,2,1,0:T(8,128)S(1)} custom-call(bf16[16,262144]{1,0:T(8,128)(2,1)} %volt.1, f32[8,512]{1,0:T(8,128)} %taps_h.1, bf16[4,2,512,1024]{3,2,1,0:T(8,128)(2,1)} %weights.1, s32[1,1024]{1,0:T(1,128)} %bitcast.3, s32[8]{0:T(128)} %delay.1, bf16[512,256]{1,0:T(8,128)(2,1)} %constant.9.chan_tab_h, ...), custom_call_target="tpu_custom_call" | custom-call | tf_op jit(solution)/shard_map/pallas_call | solution.py:566
  166.7 3.4 %copy.9 = f32[256,2,8,512]{3,2,1,0:T(8,128)} copy(f32[256,2,8,512]{3,2,1,0:T(8,128)S(1)} %bitcast.2) | data formatting | bytes 16777216

commit v3 on v2

--- a/solution.py
+++ b/solution.py
@@ -258,30 +258,36 @@
             send_a[t, pl.ds(jh * 4, 4), pl.ds(0, 4)] = moved[:, :SC].reshape(4, 4, ANT, SC)
             send_a[t, pl.ds(jh * 4, 4), pl.ds(4, 4)] = moved[:, SC:].reshape(4, 4, ANT, SC)
 
-        def send(s, pairs):
+        def send(s, r):
             dy, dz = shift(s)
-            for dx, dc in pairs:
-                to = partner((dy, dz, dx, dc))
-                pltpu.make_async_remote_copy(
-                    send_a.at[t, to],
-                    recv_a.at[t, :, mine, :],
-                    sa_send.at[t],
-                    sa_recv.at[t],
-                    device_id=(sec, to),
-                    device_id_type=MESH,
-                ).start()
+            q = (2 * s + s // NY + r) % (NX * NC)
+            to = partner((dy, dz, q // NC, q % NC))
+            pltpu.make_async_remote_copy(
+                send_a.at[t, to],
+                recv_a.at[t, :, mine, :],
+                sa_send.at[t],
+                sa_recv.at[t],
+                device_id=(sec, to),
+                device_id_type=MESH,
+            ).start()
 
         nshift = NY * NZ
         regroup(1)
 
         def step(k, carry):
             regroup(lax.rem(k + 2, nshift))
-            send(k + 1, ((1, 0), (0, 1), (1, 1), (0, 0)))
+            send(k + 1, 0)
             return carry
 
         lax.fori_loop(0, nshift - 1, step, 0)
-        send(0, ((1, 0), (0, 1), (1, 1)))
         pltpu.make_async_copy(send_a.at[t, me], recv_a.at[t, :, mine, :], sa_recv.at[t]).start()
+
+        def rest(r, carry):
+            for k in range(nshift):
+                send((k + 1) % nshift, r)
+            return carry
+
+        lax.fori_loop(1, NX * NC, rest, 0)
 
         @pl.when((i == 0) & (sec == 0))
         def _():
@@ -471,23 +477,50 @@
         to_relay.start()
         halo_b.start()
 
-    lax.fori_loop(CHUNKS - 1, CHUNKS, form, 0)
-
     @pl.when(sec == 1)
     def _():
         to_relay.wait_recv()
         forward.start()
 
-    def dedisperse(n, carry):
-        late = n // 4
-        m = (1 - late) * (3 - n // 2) + late * (1 - n % 2)
-        cp = (1 - late) * (n % 2) + late * ((n // 2) % 2)
-
-        @pl.when(m > 0)
-        def _():
-            wait_series(m - 1, cp)
-
-        @pl.when((n == 5) & (sec == 1))
+    lax.fori_loop(CHUNKS - 1, CHUNKS, form, 0)
+
+    def series_rows(slot, cp, r):
+        qs = pl.ds(r * (RT // 64), RT // 64)
+        return [recv_b[slot, cp, ri, qs].reshape(RT, SC) for ri in range(2)]
+
+    def finish(m, cp, r, spec):
+        rs = pl.ds(pl.multiple_of(r * RT, RT), RT)
+        sr, si = spec[:, :256], spec[:, 256:]
+        cr, ci = chirp[0, cp, rs, :], chirp[1, cp, rs, :]
+        filtered = jnp.concatenate(
+            [(sr * cr - si * ci).astype(BF16), (sr * ci + si * cr).astype(BF16)], axis=1
+        )
+        res = jnp.dot(filtered, inv[...], preferred_element_type=F32)
+        gs = pl.ds(r * (RT // 16), RT // 16)
+        ns = pl.ds(pl.multiple_of(m * SC, SC), SC)
+        for ri in range(2):
+            part = res[:, ri * SC : (ri + 1) * SC].reshape(RT // 16, 2, BPD, SC)
+            for cc in range(2):
+                out[gs, cp * 2 + cc, ri, :, ns] = part[:, cc]
+
+    def early(n, carry):
+        m, cp = 3 - n // 2, n % 2
+        wait_series(m - 1, cp)
+
+        def tile(r, carry):
+            block = jnp.concatenate(series_rows(m, cp, r) + series_rows(m + 1, cp, r), axis=1)
+            finish(m, cp, r, jnp.dot(block, fwd[...], preferred_element_type=F32))
+            return carry
+
+        lax.fori_loop(0, HROWS // RT, tile, 0)
+        return carry
+
+    lax.fori_loop(0, 4, early, 0)
+
+    def partial(k, carry):
+        cp, halo = k % 2, k // 2
+
+        @pl.when((k == 2) & (sec == 1))
         def _():
             halo_b.wait_recv()
             pltpu.make_async_remote_copy(
@@ -501,31 +534,48 @@
                     device_id=(sec, flip), device_id_type=MESH,
                 ).wait_recv()
 
+        slot = 2 * (1 - halo)
+        table = pl.ds(pl.multiple_of((1 - halo) * 2 * SC, 2 * SC), 2 * SC)
+
         def tile(r, carry):
             rs = pl.ds(pl.multiple_of(r * RT, RT), RT)
-            qs = pl.ds(r * (RT // 64), RT // 64)
-            block = jnp.concatenate(
-                [recv_b[m + d, cp, ri, qs].reshape(RT, SC) for d in range(2) for ri in range(2)], axis=1
-            )
-            spec = jnp.dot(block, fwd[...], preferred_element_type=F32)
-            sr, si = spec[:, :256], spec[:, 256:]
-            cr, ci = chirp[0, cp, rs, :], chirp[1, cp, rs, :]
-            filtered = jnp.concatenate(
-                [(sr * cr - si * ci).astype(BF16), (sr * ci + si * cr).astype(BF16)], axis=1
-            )
-            res = jnp.dot(filtered, inv[...], preferred_element_type=F32)
-            gs = pl.ds(r * (RT // 16), RT // 16)
-            ns = pl.ds(pl.multiple_of(m * SC, SC), SC)
-            for ri in range(2):
-                part = res[:, ri * SC : (ri + 1) * SC].reshape(RT // 16, 2, BPD, SC)
-                for cc in range(2):
-                    out[gs, cp * 2 + cc, ri, :, ns] = part[:, cc]
+            rows = jnp.concatenate(series_rows(slot, cp, r), axis=1)
+            spec = jnp.dot(rows, fwd[table, :], preferred_element_type=F32)
+            value = spec.astype(BF16)
+            rest = (spec - value.astype(F32)).astype(BF16)
+            for q in range(4):
+                recv_a[3 - k, q, rs, :] = value[:, q * 128 : (q + 1) * 128]
+                recv_a[3 - k, 4 + q, rs, :] = rest[:, q * 128 : (q + 1) * 128]
             return carry
 
         lax.fori_loop(0, HROWS // RT, tile, 0)
         return carry
 
-    lax.fori_loop(0, 2 * CHUNKS, dedisperse, 0)
+    lax.fori_loop(0, 4, partial, 0)
+
+    def late(cp, carry):
+        wait_series(0, cp)
+
+        def tile(r, carry):
+            rs = pl.ds(pl.multiple_of(r * RT, RT), RT)
+
+            def kept(k):
+                return jnp.concatenate(
+                    [recv_a[k, q, rs, :].astype(F32) + recv_a[k, 4 + q, rs, :].astype(F32) for q in range(4)],
+                    axis=1,
+                )
+
+            rows = jnp.concatenate(series_rows(1, cp, r), axis=1)
+            spec = jnp.dot(rows, fwd[pl.ds(0, 2 * SC), :], preferred_element_type=F32)
+            odd = lax.broadcasted_iota(jnp.int32, (RT, 512), 1) % 2 == 1
+            finish(1, cp, r, spec + kept(3 - cp))
+            finish(0, cp, r, jnp.where(odd, -spec, spec) + kept(1 - cp))
+            return carry
+
+        lax.fori_loop(0, HROWS // RT, tile, 0)
+        return carry
+
+    lax.fori_loop(0, 2, late, 0)
 
     @pl.when(sec == 0)
     def _():

time: 171 us -> 166 us (0.971); the launches traced: 170 us -> 163 us
  Pallas kernels: 167 us -> 159 us
    pallas_call x1, Pallas kernels: 167 us -> 159 us  [local(): pl.pallas_call(kernel, out_shape=pltpu.VMEM((NG, CPD, 2, BPD, CHUNKS * SC...]
where the time goes in v3:
time: 166 us; the launch traced here: 163 us
  Pallas kernels  159 us (96%)
  local copies, waits for them, and re-layouts  3.4 us (2%)
    pallas_call x1, Pallas kernels, local(): pl.pallas_call(kernel, out_shape=pltpu.VMEM((NG, CPD, 2, BPD, CHUNKS * SC...  159 us
    unnamed x1, local copies, waits for them, and re-layouts  3.4 us

profile of v3, /device:TPU:4, one launch (start us, length us, event | category | flops | bytes accessed | tf_op | source)
XLA Modules:
  0.0 162.6 jit_solution(14445155436906472592)
XLA Ops:
  0.0 159.2 %shard_map.73 = f32[64,4,2,8,512]{4,3,2,1,0:T(8,128)S(1)} custom-call(bf16[16,262144]{1,0:T(8,128)(2,1)} %volt.1, f32[8,512]{1,0:T(8,128)} %taps_h.1, bf16[4,2,512,1024]{3,2,1,0:T(8,128)(2,1)} %weights.1, s32[1,1024]{1,0:T(1,128)} %bitcast.3, s32[8]{0:T(128)} %delay.1, bf16[512,256]{1,0:T(8,128)(2,1)} %constant.9.chan_tab_h, ...), custom_call_target="tpu_custom_call" | custom-call | tf_op jit(solution)/shard_map/pallas_call | solution.py:616
  159.2 3.4 %copy.9 = f32[256,2,8,512]{3,2,1,0:T(8,128)} copy(f32[256,2,8,512]{3,2,1,0:T(8,128)S(1)} %bitcast.2) | data formatting | bytes 16777216

commit v4 on v3

--- a/solution.py
+++ b/solution.py
@@ -30,7 +30,7 @@
 ALL_ANT = ANT * NG
 HROWS = ROWS // 2
 RT = 256
-VMEM_LIMIT = 55 * 2**20
+VMEM_LIMIT = 41 * 2**20
 
 
 def send_order(seed=0):
@@ -88,11 +88,63 @@
     return np.stack([np.cos(angle) * factor, np.sin(angle) * factor]).astype(np.float32)
 
 
+def disperse_back(spec, chirp, inv, cp, r):
+    rs = pl.ds(pl.multiple_of(r * RT, RT), RT)
+    sr, si = spec[:, :256], spec[:, 256:]
+    cr, ci = chirp[0, cp, rs, :], chirp[1, cp, rs, :]
+    filtered = jnp.concatenate([(sr * cr - si * ci).astype(BF16), (sr * ci + si * cr).astype(BF16)], axis=1)
+    return jnp.dot(filtered, inv[...], preferred_element_type=F32)
+
+
+def last_blocks(rows, kept, chirp, fwd, inv, cp, r):
+    rs = pl.ds(pl.multiple_of(r * RT, RT), RT)
+
+    def part(k):
+        return jnp.concatenate(
+            [kept[k, q, rs, :].astype(F32) + kept[k, 4 + q, rs, :].astype(F32) for q in range(4)], axis=1
+        )
+
+    spec = jnp.dot(rows, fwd[pl.ds(0, 2 * SC), :], preferred_element_type=F32)
+    odd = lax.broadcasted_iota(jnp.int32, (RT, 512), 1) % 2 == 1
+    return (
+        disperse_back(jnp.where(odd, -spec, spec) + part(1 - cp), chirp, inv, cp, r),
+        disperse_back(spec + part(3 - cp), chirp, inv, cp, r),
+    )
+
+
+def finish_kernel(done, kept, chirp, fwd, inv, z_last, out, obuf, sem):
+    news = pl.ds(2 * SC, 2 * SC)
+    olds = pl.ds(0, 2 * SC)
+    copies = [
+        pltpu.make_async_copy(done.at[:, :, :, :, news], out.at[:, :, :, :, news], sem.at[0]),
+        pltpu.make_async_copy(
+            done.at[:, pl.ds(0, 2), :, :, olds], out.at[:, pl.ds(0, 2), :, :, olds], sem.at[1]
+        ),
+    ]
+    for copy in copies:
+        copy.start()
+    for r in range(HROWS // RT):
+        rows = jnp.concatenate([z_last[ri, pl.ds(r * RT, RT), :] for ri in range(2)], axis=1)
+        gs = pl.ds(r * (RT // 16), RT // 16)
+        for m, res in enumerate(last_blocks(rows, kept, chirp, fwd, inv, 1, r)):
+            for ri in range(2):
+                part = res[:, ri * SC : (ri + 1) * SC].reshape(RT // 16, 2, BPD, SC)
+                for cc in range(2):
+                    obuf[gs, cc, ri, :, pl.ds(m * SC, SC)] = part[:, cc]
+        copy = pltpu.make_async_copy(
+            obuf.at[gs], out.at[gs, pl.ds(2, 2), :, :, olds], sem.at[2 + r]
+        )
+        copy.start()
+        copies.append(copy)
+    for copy in copies:
+        copy.wait()
+
+
 def kernel(
     volt, taps_h, weights, ant_row_h, delay, chan_tab_h, blk_tab_h,
-    out,
-    vbuf, halo_a, wblk, wrow, chan, send_a, recv_a, perm, onehot, wstage, wperm,
-    btmp, send_b, recv_b, relay, chirp, fwd, inv, taps, ant_row, chan_tab, blk_tab,
+    out, recv_a, chirp, fwd, inv, z_last,
+    vbuf, halo_a, wblk, wrow, chan, send_a, perm, onehot, wstage, wperm,
+    btmp, send_b, recv_b, relay, taps, ant_row, chan_tab, blk_tab,
     sem_v, sem_w, sem_t, sem_ha, sem_hb, sem_rl, sem_fw, sem_mc, sa_send, sa_recv, sb_send, sb_recv,
 ):
     sec = lax.axis_index("section")
@@ -488,14 +540,7 @@
         qs = pl.ds(r * (RT // 64), RT // 64)
         return [recv_b[slot, cp, ri, qs].reshape(RT, SC) for ri in range(2)]
 
-    def finish(m, cp, r, spec):
-        rs = pl.ds(pl.multiple_of(r * RT, RT), RT)
-        sr, si = spec[:, :256], spec[:, 256:]
-        cr, ci = chirp[0, cp, rs, :], chirp[1, cp, rs, :]
-        filtered = jnp.concatenate(
-            [(sr * cr - si * ci).astype(BF16), (sr * ci + si * cr).astype(BF16)], axis=1
-        )
-        res = jnp.dot(filtered, inv[...], preferred_element_type=F32)
+    def store(m, cp, r, res):
         gs = pl.ds(r * (RT // 16), RT // 16)
         ns = pl.ds(pl.multiple_of(m * SC, SC), SC)
         for ri in range(2):
@@ -509,7 +554,8 @@
 
         def tile(r, carry):
             block = jnp.concatenate(series_rows(m, cp, r) + series_rows(m + 1, cp, r), axis=1)
-            finish(m, cp, r, jnp.dot(block, fwd[...], preferred_element_type=F32))
+            spec = jnp.dot(block, fwd[...], preferred_element_type=F32)
+            store(m, cp, r, disperse_back(spec, chirp, inv, cp, r))
             return carry
 
         lax.fori_loop(0, HROWS // RT, tile, 0)
@@ -553,29 +599,18 @@
 
     lax.fori_loop(0, 4, partial, 0)
 
-    def late(cp, carry):
-        wait_series(0, cp)
-
-        def tile(r, carry):
-            rs = pl.ds(pl.multiple_of(r * RT, RT), RT)
-
-            def kept(k):
-                return jnp.concatenate(
-                    [recv_a[k, q, rs, :].astype(F32) + recv_a[k, 4 + q, rs, :].astype(F32) for q in range(4)],
-                    axis=1,
-                )
-
-            rows = jnp.concatenate(series_rows(1, cp, r), axis=1)
-            spec = jnp.dot(rows, fwd[pl.ds(0, 2 * SC), :], preferred_element_type=F32)
-            odd = lax.broadcasted_iota(jnp.int32, (RT, 512), 1) % 2 == 1
-            finish(1, cp, r, spec + kept(3 - cp))
-            finish(0, cp, r, jnp.where(odd, -spec, spec) + kept(1 - cp))
-            return carry
-
-        lax.fori_loop(0, HROWS // RT, tile, 0)
+    wait_series(0, 0)
+
+    def late(r, carry):
+        rows = jnp.concatenate(series_rows(1, 0, r), axis=1)
+        for m, res in enumerate(last_blocks(rows, recv_a, chirp, fwd, inv, 0, r)):
+            store(m, 0, r, res)
         return carry
 
-    lax.fori_loop(0, 2, late, 0)
+    lax.fori_loop(0, HROWS // RT, late, 0)
+    wait_series(0, 1)
+    for ri in range(2):
+        z_last[ri] = recv_b[1, 1, ri].reshape(HROWS, SC)
 
     @pl.when(sec == 0)
     def _():
@@ -615,9 +650,16 @@
     dma = pltpu.SemaphoreType.DMA
     series = pl.pallas_call(
         kernel,
-        out_shape=pltpu.VMEM((NG, CPD, 2, BPD, CHUNKS * SC), F32),
+        out_shape=[
+            pltpu.VMEM((NG, CPD, 2, BPD, CHUNKS * SC), F32),
+            pltpu.VMEM((CHUNKS, 2 * CPD, ALL_ANT, SC), BF16),
+            pltpu.VMEM((2, 2, HROWS, 256), F32),
+            pltpu.VMEM((512, 512), BF16),
+            pltpu.VMEM((512, 256), BF16),
+            pltpu.VMEM((2, HROWS, SC), BF16),
+        ],
         in_specs=[hbm, hbm, hbm, hbm, smem, hbm, hbm],
-        out_specs=vmem,
+        out_specs=[vmem] * 6,
         scratch_shapes=[
             pltpu.VMEM((2, ANT, SC * FRAME + LEAD), BF16),
             pltpu.VMEM((ANT, LEAD), BF16),
@@ -625,7 +667,6 @@
             pltpu.VMEM((ANT, SC, FRAME), BF16),
             pltpu.VMEM((2, ANT, 256, SC), BF16),
             pltpu.VMEM((CHUNKS, NG, 2 * CPD, ANT, SC), BF16),
-            pltpu.VMEM((CHUNKS, 2 * CPD, ALL_ANT, SC), BF16),
             pltpu.VMEM((256, 256), BF16),
             pltpu.VMEM((ALL_ANT, ALL_ANT), BF16),
             pltpu.VMEM((2, BEAMS, ALL_ANT), BF16),
@@ -634,9 +675,6 @@
             pltpu.VMEM((CHUNKS, 2, 2, NG, 16, SC), BF16),
             pltpu.VMEM((CHUNKS + 1, 2, 2, NY * NZ, NX, 32, SC), BF16),
             pltpu.VMEM((2, NY * NZ, 32, SC), BF16),
-            pltpu.VMEM((2, 2, HROWS, 256), F32),
-            pltpu.VMEM((512, 512), BF16),
-            pltpu.VMEM((512, 256), BF16),
             pltpu.VMEM((TAPS, FRAME), F32),
             pltpu.VMEM((1, ALL_ANT), jnp.int32),
             pltpu.VMEM((512, HALF), BF16),
@@ -648,7 +686,15 @@
             collective_id=0, has_side_effects=True, vmem_limit_bytes=VMEM_LIMIT
         ),
     )(voltages, filter_taps, beam_weights, ant_row, beam_delay, chan_tab, blk_tab)
-    return series.reshape(CH, 2, BPD, CHUNKS * SC)
+    result = pl.pallas_call(
+        finish_kernel,
+        out_shape=jax.ShapeDtypeStruct((NG, CPD, 2, BPD, CHUNKS * SC), F32),
+        in_specs=[vmem] * 6,
+        out_specs=hbm,
+        scratch_shapes=[pltpu.VMEM((NG, 2, 2, BPD, 2 * SC), F32), dma((2 + HROWS // RT,))],
+        compiler_params=pltpu.CompilerParams(vmem_limit_bytes=8 * 2**20),
+    )(*series)
+    return result.reshape(CH, 2, BPD, CHUNKS * SC)
 
 
 def solution(mesh):

time: 166 us -> 163 us (0.982)
  local copies, waits for them, and re-layouts: 3.4 us -> 0 us
    unnamed x1 -> x0, local copies, waits for them, and re-layouts: 3.4 us -> none
    pallas_call x1 -> x2, Pallas kernels: 159 us -> 160 us  [the longest x1 157 us: local(): pl.pallas_call(kernel, out_shape=[pltpu.VMEM((NG, CPD, 2, BPD, CHUNKS * S...]
where the time goes in v4:
time: 163 us; the launch traced here: 160 us
  Pallas kernels  160 us (98%)
    pallas_call x1, Pallas kernels, local(): pl.pallas_call(kernel, out_shape=[pltpu.VMEM((NG, CPD, 2, BPD, CHUNKS * S...  157 us
    pallas_call x1, Pallas kernels, local(): pl.pallas_call(finish_kernel, out_shape=jax.ShapeDtypeStruct((NG, CPD, 2,...  3.33 us

profile of v4, /device:TPU:4, one launch (start us, length us, event | category | flops | bytes accessed | tf_op | source)
XLA Modules:
  0.0 160.2 jit_solution(11735224972128052411)
XLA Ops:
  0.0 156.8 %shard_map.73 = (f32[64,4,2,8,512]{4,3,2,1,0:T(8,128)S(1)}, bf16[4,8,1024,128]{3,2,1,0:T(8,128)(2,1)S(1)}, f32[2,2,1024,256]{3,2,1,0:T(8,128)S(1)}, bf16[512,512...) custom-call(bf16[16,262144]{1,0:T(8,128)(2,1)} %volt.1, f32[8,512]{1,0:T(8,128)} %taps_h.1, ...), custom_call_target="tpu_custom_call" | custom-call | tf_op jit(solution)/shard_map/pallas_call | solution.py:651
  156.8 3.3 %shard_map.74 = f32[64,4,2,8,512]{4,3,2,1,0:T(8,128)} custom-call(f32[64,4,2,8,512]{4,3,2,1,0:T(8,128)S(1)} %get-tuple-element.11.done, bf16[4,8,1024,128]{3,2,1,0:T(8,128)(2,1)S(1)} %get-tuple-element.12.kept, f32[2,2,1024,256]{3,2,1,0:T(8,128)S(1)} %get-tuple-element.13.chirp, bf16[512,512]{1,0:T(8,128)(2,1)S(1)} %get-tuple-element.14.fwd, ...), custom_call_target="tpu_custom_call" | custom-call | tf_op jit(solution)/shard_map/pallas_call | solution.py:689

commit v5 on v4

--- a/solution.py
+++ b/solution.py
@@ -145,7 +145,7 @@
     out, recv_a, chirp, fwd, inv, z_last,
     vbuf, halo_a, wblk, wrow, chan, send_a, perm, onehot, wstage, wperm,
     btmp, send_b, recv_b, relay, taps, ant_row, chan_tab, blk_tab,
-    sem_v, sem_w, sem_t, sem_ha, sem_hb, sem_rl, sem_fw, sem_mc, sa_send, sa_recv, sb_send, sb_recv,
+    sem_v, sem_first, sem_w, sem_t, sem_ha, sem_hb, sem_rl, sem_fw, sem_mc, sa_send, sa_recv, sb_send, sb_recv,
 ):
     sec = lax.axis_index("section")
     me = lax.axis_index("grp")
@@ -170,6 +170,14 @@
             sem_v.at[(CHUNKS - 1) % 2],
         )
 
+    def load_first(n):
+        start, size = (0, LEAD + SC * FRAME // 4) if n == 0 else (LEAD + n * (SC * FRAME // 4), SC * FRAME // 4)
+        return pltpu.make_async_copy(
+            volt.at[:, pl.ds((CHUNKS - 1) * (SC * FRAME) - LEAD + start, size)],
+            vbuf.at[0, :, pl.ds(start, size)],
+            sem_first.at[n],
+        )
+
     def load_w(k):
         return pltpu.make_async_copy(
             weights.at[k // 2, lax.rem(k, 2)], wstage.at[lax.rem(k, 2)], sem_w.at[lax.rem(k, 2)]
@@ -182,9 +190,11 @@
         )
     ]
 
-    load_v(0).start()
+    load_first(0).start()
     for copy in small:
         copy.start()
+    for n in range(1, 4):
+        load_first(n).start()
     load_w(0).start()
     barrier = pltpu.get_barrier_semaphore()
     for o in ORDER:
@@ -198,7 +208,6 @@
     perm[...] = jnp.where((row % 16) * 16 + row // 16 == col, 1.0, 0.0).astype(BF16)
     wblk[...] = jnp.zeros_like(wblk)
     small[0].wait()
-    small[1].wait()
 
     halo_copy = pltpu.make_async_remote_copy(
         volt.at[:, pl.ds(CHUNKS * SC * FRAME - LEAD, LEAD)],
@@ -248,7 +257,7 @@
         def _():
             load_v0().start()
 
-        @pl.when(i < CHUNKS - 1)
+        @pl.when((i > 0) & (i < CHUNKS - 1))
         def _():
             load_v(i).wait()
 
@@ -263,6 +272,12 @@
             vbuf[(CHUNKS - 1) % 2, :, pl.ds(0, LEAD)] = halo_a[...]
 
         def fir(sb, carry):
+            for n in range(4):
+
+                @pl.when((i == 0) & (sb == 2 * n))
+                def _():
+                    load_first(n).wait()
+
             moved = move_rows(lax.rem(sb + 1, 2))
             fir_block(slot, sb, lax.rem(sb, 2))
             before = pl.multiple_of(jnp.maximum(sb - 1, 0) * 16, 16)
@@ -272,6 +287,10 @@
         nblk = SC // 16
         lax.fori_loop(0, nblk, fir, 0)
         wrow[:, pl.ds((nblk - 1) * 16, 16), :] = move_rows((nblk - 1) % 2)
+
+        @pl.when(i == 0)
+        def _():
+            small[1].wait()
 
         def dft(ap2, carry):
             for u in range(2):
@@ -679,7 +698,7 @@
             pltpu.VMEM((1, ALL_ANT), jnp.int32),
             pltpu.VMEM((512, HALF), BF16),
             pltpu.VMEM((2, 256, 256), BF16),
-            dma((2,)), dma((2,)), dma((4,)), dma((2,)), dma((2,)), dma((2,)), dma((2,)), dma((2, 2)),
+            dma((2,)), dma((4,)), dma((2,)), dma((4,)), dma((2,)), dma((2,)), dma((2,)), dma((2,)), dma((2, 2)),
             dma((CHUNKS,)), dma((CHUNKS,)), dma((CHUNKS, 2)), dma((CHUNKS, 2)),
         ],
         compiler_params=pltpu.CompilerParams(

time: 163 us -> 163 us (level)
  no operation moved by 1% of the time
where the time goes in v5:
time: 163 us; the launch traced here: 159 us
  Pallas kernels  159 us (98%)
    pallas_call x1, Pallas kernels, local(): pl.pallas_call(kernel, out_shape=[pltpu.VMEM((NG, CPD, 2, BPD, CHUNKS * S...  156 us
    pallas_call x1, Pallas kernels, local(): pl.pallas_call(finish_kernel, out_shape=jax.ShapeDtypeStruct((NG, CPD, 2,...  3.33 us

profile of v5, /device:TPU:4, one launch (start us, length us, event | category | flops | bytes accessed | tf_op | source)
XLA Modules:
  0.0 159.5 jit_solution(10138603827519256638)
XLA Ops:
  0.0 156.1 %shard_map.73 = (f32[64,4,2,8,512]{4,3,2,1,0:T(8,128)S(1)}, bf16[4,8,1024,128]{3,2,1,0:T(8,128)(2,1)S(1)}, f32[2,2,1024,256]{3,2,1,0:T(8,128)S(1)}, bf16[512,512...) custom-call(bf16[16,262144]{1,0:T(8,128)(2,1)} %volt.1, f32[8,512]{1,0:T(8,128)} %taps_h.1, ...), custom_call_target="tpu_custom_call" | custom-call | tf_op jit(solution)/shard_map/pallas_call | solution.py:670
  156.1 3.3 %shard_map.74 = f32[64,4,2,8,512]{4,3,2,1,0:T(8,128)} custom-call(f32[64,4,2,8,512]{4,3,2,1,0:T(8,128)S(1)} %get-tuple-element.11.done, bf16[4,8,1024,128]{3,2,1,0:T(8,128)(2,1)S(1)} %get-tuple-element.12.kept, f32[2,2,1024,256]{3,2,1,0:T(8,128)S(1)} %get-tuple-element.13.chirp, bf16[512,512]{1,0:T(8,128)(2,1)S(1)} %get-tuple-element.14.fwd, ...), custom_call_target="tpu_custom_call" | custom-call | tf_op jit(solution)/shard_map/pallas_call | solution.py:708
